TPU v7x, 64 devices: a 2x2x8 block of a 4x4x8 slice. The times are simulated.
64 devices in a mesh: data: 4 (over x, y), time: 16 (over z, core).
Axes of the slice: x: 2, y: 2, z: 8, core: 2. Of those that a mesh axis runs over, the one named last changes fastest.
The devices are a block of a 4x4x8 slice.
Arguments:
- x_init: float32 [32, 1024, 16], P('data'), parts along dimension 0
- w_in: bfloat16 [16, 1152], replicated
- w_out: bfloat16 [1152, 16], replicated
- mod_scale: bfloat16 [16, 1152], P('time')
- mod_shift: bfloat16 [16, 1152], P('time')
- step_size: float32 [16], P('time')
Outputs:
- output: float32 [16, 32, 1024, 16], P('time', 'data'), parts along dimension 1
There are 4 independent parts. A program takes and returns all parts, laid end to end along the dimension named above; an argument that names none is the same for every part.
All inputs are finite; a program needn't handle non-finite values.
Results may differ from a plain program's by a relative error of at most 0.001.
Values are sent between devices in bfloat16 or wider.
A program may use at most 768 MiB of HBM per device.

v0:
```python
import jax
import jax.numpy as jnp
from jax import lax
from jax.sharding import PartitionSpec as P

SWEEPS = 4


def drift_block(pre_act, scale, shift, w_out):
    hidden_act = jax.nn.gelu(pre_act * scale + shift, approximate=True)
    return jnp.einsum("kbnd,dc->kbnc", hidden_act.astype(jnp.bfloat16), w_out, preferred_element_type=jnp.float32)


def solution(mesh):
    n_time = mesh.shape["time"]
    from_next = [(source, source - 1) for source in range(1, n_time)]
    hop_dists = [2 ** power for power in range(n_time) if 2 ** power < n_time]

    def local(x_init, w_in, w_out, mod_scale, mod_shift, step_size):
        scale = (1.0 + mod_scale.astype(jnp.float32))[:, None, None, :]
        shift = mod_shift.astype(jnp.float32)[:, None, None, :]
        pre_act = jnp.einsum("bnc,cd->bnd", x_init.astype(jnp.bfloat16), w_in, preferred_element_type=jnp.float32)[None]
        latents = None
        for sweep in range(SWEEPS):
            if sweep > 0:
                pre_act = jnp.einsum("kbnc,cd->kbnd", latents.astype(jnp.bfloat16), w_in, preferred_element_type=jnp.float32)
            drifts = drift_block(pre_act, scale, shift, w_out)
            next_first = lax.ppermute(drifts[0], "time", from_next)
            next_drifts = jnp.concatenate([drifts[1:], next_first[None]], axis=0)
            increments = step_size[:, None, None, None] * (0.5 * (drifts + next_drifts))
            local_cum = jnp.cumsum(increments, axis=0)
            local_excl = jnp.concatenate([jnp.zeros_like(local_cum[:1]), local_cum[:-1]], axis=0)
            dev_total = local_cum[-1]
            inclusive = dev_total
            for distance in hop_dists:
                inclusive = inclusive + lax.ppermute(inclusive, "time", [(source, source + distance) for source in range(n_time - distance)])
            offset = inclusive - dev_total
            latents = x_init[None] + (offset[None] + local_excl)
        return latents

    return jax.shard_map(local, mesh=mesh, in_specs=(P("data"), P(), P(), P("time"), P("time"), P("time")), out_specs=P("time", "data"), check_vma=False)
```

profile of v0, /device:TPU:54, one launch (start us, length us, event | category | flops | bytes accessed | tf_op | source)
XLA Modules:
  0.0 435.3 jit_solution(10983925950799301796)
XLA Ops:
  0.0 0.7 convert_reduce_fusion
  0.8 17.4 %fusion.35 = f32[8,1024,16]{1,2,0:T(8,128)S(1)} fusion(f32[1152]{0:T(1024)S(1)} %get-tuple-element.5, f32[1152]{0:T(1024)S(1)} %get-tuple-element.6, f32[8,1024,16]{1,2,0:T(8,128)} %param.6, bf16[1152,16]{0,1:T(8,128)(2,1)S(1)} %copy-done, bf16[16,1152]{1,0:T(8,128)(2,1)} %param.7), kind=kOutput, calls=%fused_computation.39 | convolution fusion | flops 707919872 | bytes 1131520 | tf_op jit(solution)/shard_map/kbnd,dc->kbnc/dot_general | solution.py:11
  18.2 2.0 collective-permute-start
  20.8 6.0 %collective-permute-done = f32[8,1024,16]{1,2,0:T(8,128)S(1)} collective-permute-done((f32[8,1024,16]{1,2,0:T(8,128)S(1)}, f32[8,1024,16]{1,2,0:T(8,128)S(1)}, u32[]{:S(2)}, u32[]{:S(2)}) %collective-permute-start) | collective-permute-done | bytes 524320 | tf_op jit(solution)/shard_map/ppermute | solution.py:28
  26.8 0.1 add_multiply_fusion.3
  26.9 4.4 collective-permute-start.1
  31.2 6.4 %collective-permute-done.1 = f32[8,1024,16]{1,2,0:T(8,128)S(1)} collective-permute-done((f32[8,1024,16]{1,2,0:T(8,128)S(1)}, f32[8,1024,16]{1,2,0:T(8,128)S(1)}, u32[]{:S(2)}, u32[]{:S(2)}) %collective-permute-start.1) | collective-permute-done | bytes 524320 | tf_op jit(solution)/shard_map/ppermute | solution.py:36
  37.7 4.1 collective-permute-start.2
  41.7 11.4 %collective-permute-done.2 = f32[8,1024,16]{1,2,0:T(8,128)S(1)} collective-permute-done((f32[8,1024,16]{1,2,0:T(8,128)S(1)}, f32[8,1024,16]{1,2,0:T(8,128)S(1)}, u32[]{:S(2)}, u32[]{:S(2)}) %collective-permute-start.2) | collective-permute-done | bytes 524320 | tf_op jit(solution)/shard_map/ppermute | solution.py:36
  53.3 7.0 %collective-permute-start.3 = (f32[8,1024,16]{1,2,0:T(8,128)S(1)}, f32[8,1024,16]{1,2,0:T(8,128)S(1)}, u32[]{:S(2)}, u32[]{:S(2)}) collective-permute-start(f32[8,1024,16]{1,2,0:T(8,128)S(1)} %add.172), channel_id=1, source_target_pairs={{0,4},{1,5},{2,6},{3,7},{4,8},{5,9},{6,10},{7,11},{8,12},{9,13},{1... | collective-permute-start | bytes 1572872 | tf_op jit(solution)/shard_map/ppermute | solution.py:36
  60.2 33.8 %collective-permute-done.3 = f32[8,1024,16]{1,2,0:T(8,128)S(1)} collective-permute-done((f32[8,1024,16]{1,2,0:T(8,128)S(1)}, f32[8,1024,16]{1,2,0:T(8,128)S(1)}, u32[]{:S(2)}, u32[]{:S(2)}) %collective-permute-start.3) | collective-permute-done | bytes 524320 | tf_op jit(solution)/shard_map/ppermute | solution.py:36
  94.1 7.0 %collective-permute-start.4 = (f32[8,1024,16]{1,2,0:T(8,128)S(1)}, f32[8,1024,16]{1,2,0:T(8,128)S(1)}, u32[]{:S(2)}, u32[]{:S(2)}) collective-permute-start(f32[8,1024,16]{1,2,0:T(8,128)S(1)} %add.173), channel_id=1, source_target_pairs={{0,8},{1,9},{2,10},{3,11},{4,12},{5,13},{6,14},{7,15},{16,24},{17,... | collective-permute-start | bytes 1572872 | tf_op jit(solution)/shard_map/ppermute | solution.py:36
  101.0 20.6 %collective-permute-done.4 = f32[8,1024,16]{1,2,0:T(8,128)S(1)} collective-permute-done((f32[8,1024,16]{1,2,0:T(8,128)S(1)}, f32[8,1024,16]{1,2,0:T(8,128)S(1)}, u32[]{:S(2)}, u32[]{:S(2)}) %collective-permute-start.4) | collective-permute-done | bytes 524320 | tf_op jit(solution)/shard_map/ppermute | solution.py:36
  121.6 16.5 %fusion.34 = f32[8,1024,16]{1,2,0:T(8,128)S(1)} fusion(f32[1152]{0:T(1024)S(1)} %get-tuple-element.5, f32[1152]{0:T(1024)S(1)} %get-tuple-element.6, f32[8,1024,16]{1,2,0:T(8,128)S(1)} %copy-done.1, f32[8,1024,16]{1,2,0:T(8,128)S(1)} %add_multiply_fusion.3, f32[8,1024,16]{1,2,0:T(8,128)S(1)} %add.173, f32[8,1024,16]{1,2,0:T(8,128)S(1)} %collective-permute-done.4, ...), kind=kOutput, calls=%fused_computation.38 | convolution fusion | flops 708313088 | bytes 2704384 | tf_op jit(solution)/shard_map/kbnd,dc->kbnc/dot_general | solution.py:11
  138.1 2.0 collective-permute-start.5
  140.1 6.7 %collective-permute-done.5 = f32[8,1024,16]{1,2,0:T(8,128)S(1)} collective-permute-done((f32[8,1024,16]{1,2,0:T(8,128)S(1)}, f32[8,1024,16]{1,2,0:T(8,128)S(1)}, u32[]{:S(2)}, u32[]{:S(2)}) %collective-permute-start.5) | collective-permute-done | bytes 524320 | tf_op jit(solution)/shard_map/ppermute | solution.py:28
  146.8 4.0 collective-permute-start.6
  150.8 6.8 %collective-permute-done.6 = f32[8,1024,16]{1,2,0:T(8,128)S(1)} collective-permute-done((f32[8,1024,16]{1,2,0:T(8,128)S(1)}, f32[8,1024,16]{1,2,0:T(8,128)S(1)}, u32[]{:S(2)}, u32[]{:S(2)}) %collective-permute-start.6) | collective-permute-done | bytes 524320 | tf_op jit(solution)/shard_map/ppermute | solution.py:36
  157.6 3.7 collective-permute-start.7
  161.3 11.4 %collective-permute-done.7 = f32[8,1024,16]{1,2,0:T(8,128)S(1)} collective-permute-done((f32[8,1024,16]{1,2,0:T(8,128)S(1)}, f32[8,1024,16]{1,2,0:T(8,128)S(1)}, u32[]{:S(2)}, u32[]{:S(2)}) %collective-permute-start.7) | collective-permute-done | bytes 524320 | tf_op jit(solution)/shard_map/ppermute | solution.py:36
  172.7 1.3 collective-permute-start.8
  174.1 21.4 %collective-permute-done.8 = f32[8,1024,16]{1,2,0:T(8,128)S(1)} collective-permute-done((f32[8,1024,16]{1,2,0:T(8,128)S(1)}, f32[8,1024,16]{1,2,0:T(8,128)S(1)}, u32[]{:S(2)}, u32[]{:S(2)}) %collective-permute-start.8) | collective-permute-done | bytes 524320 | tf_op jit(solution)/shard_map/ppermute | solution.py:36
  195.6 7.9 %collective-permute-start.9 = (f32[8,1024,16]{1,2,0:T(8,128)S(1)}, f32[8,1024,16]{1,2,0:T(8,128)S(1)}, u32[]{:S(2)}, u32[]{:S(2)}) collective-permute-start(f32[8,1024,16]{1,2,0:T(8,128)S(1)} %add.182), channel_id=1, source_target_pairs={{0,8},{1,9},{2,10},{3,11},{4,12},{5,13},{6,14},{7,15},{16,24},{17,... | collective-permute-start | bytes 1572872 | tf_op jit(solution)/shard_map/ppermute | solution.py:36
  203.4 22.4 %collective-permute-done.9 = f32[8,1024,16]{1,2,0:T(8,128)S(1)} collective-permute-done((f32[8,1024,16]{1,2,0:T(8,128)S(1)}, f32[8,1024,16]{1,2,0:T(8,128)S(1)}, u32[]{:S(2)}, u32[]{:S(2)}) %collective-permute-start.9) | collective-permute-done | bytes 524320 | tf_op jit(solution)/shard_map/ppermute | solution.py:36
  225.8 16.4 %fusion.33 = f32[8,1024,16]{1,2,0:T(8,128)S(1)} fusion(f32[1152]{0:T(1024)S(1)} %get-tuple-element.5, f32[1152]{0:T(1024)S(1)} %get-tuple-element.6, f32[8,1024,16]{1,2,0:T(8,128)S(1)} %copy-done.1, f32[8,1024,16]{1,2,0:T(8,128)S(1)} %add_multiply_fusion.2, f32[8,1024,16]{1,2,0:T(8,128)S(1)} %add.182, f32[8,1024,16]{1,2,0:T(8,128)S(1)} %collective-permute-done.9, ...), kind=kOutput, calls=%fused_computation.37 | convolution fusion | flops 708313088 | bytes 2704384 | tf_op jit(solution)/shard_map/kbnd,dc->kbnc/dot_general | solution.py:11
  242.3 2.0 collective-permute-start.10
  244.2 6.7 %collective-permute-done.10 = f32[8,1024,16]{1,2,0:T(8,128)S(1)} collective-permute-done((f32[8,1024,16]{1,2,0:T(8,128)S(1)}, f32[8,1024,16]{1,2,0:T(8,128)S(1)}, u32[]{:S(2)}, u32[]{:S(2)}) %collective-permute-start.10) | collective-permute-done | bytes 524320 | tf_op jit(solution)/shard_map/ppermute | solution.py:28
  251.0 2.9 collective-permute-start.11
  253.9 7.8 %collective-permute-done.11 = f32[8,1024,16]{1,2,0:T(8,128)S(1)} collective-permute-done((f32[8,1024,16]{1,2,0:T(8,128)S(1)}, f32[8,1024,16]{1,2,0:T(8,128)S(1)}, u32[]{:S(2)}, u32[]{:S(2)}) %collective-permute-start.11) | collective-permute-done | bytes 524320 | tf_op jit(solution)/shard_map/ppermute | solution.py:36
  261.8 2.6 collective-permute-start.12
  264.4 11.4 %collective-permute-done.12 = f32[8,1024,16]{1,2,0:T(8,128)S(1)} collective-permute-done((f32[8,1024,16]{1,2,0:T(8,128)S(1)}, f32[8,1024,16]{1,2,0:T(8,128)S(1)}, u32[]{:S(2)}, u32[]{:S(2)}) %collective-permute-start.12) | collective-permute-done | bytes 524320 | tf_op jit(solution)/shard_map/ppermute | solution.py:36
  275.8 1.3 collective-permute-start.13
  277.2 21.4 %collective-permute-done.13 = f32[8,1024,16]{1,2,0:T(8,128)S(1)} collective-permute-done((f32[8,1024,16]{1,2,0:T(8,128)S(1)}, f32[8,1024,16]{1,2,0:T(8,128)S(1)}, u32[]{:S(2)}, u32[]{:S(2)}) %collective-permute-start.13) | collective-permute-done | bytes 524320 | tf_op jit(solution)/shard_map/ppermute | solution.py:36
  298.7 6.5 %collective-permute-start.14 = (f32[8,1024,16]{1,2,0:T(8,128)S(1)}, f32[8,1024,16]{1,2,0:T(8,128)S(1)}, u32[]{:S(2)}, u32[]{:S(2)}) collective-permute-start(f32[8,1024,16]{1,2,0:T(8,128)S(1)} %add.191), channel_id=1, source_target_pairs={{0,8},{1,9},{2,10},{3,11},{4,12},{5,13},{6,14},{7,15},{16,24},{17,... | collective-permute-start | bytes 1572872 | tf_op jit(solution)/shard_map/ppermute | solution.py:36
  305.2 20.9 %collective-permute-done.14 = f32[8,1024,16]{1,2,0:T(8,128)S(1)} collective-permute-done((f32[8,1024,16]{1,2,0:T(8,128)S(1)}, f32[8,1024,16]{1,2,0:T(8,128)S(1)}, u32[]{:S(2)}, u32[]{:S(2)}) %collective-permute-start.14) | collective-permute-done | bytes 524320 | tf_op jit(solution)/shard_map/ppermute | solution.py:36
  326.1 16.4 %fusion.32 = f32[8,1024,16]{1,2,0:T(8,128)S(1)} fusion(f32[1152]{0:T(1024)S(1)} %get-tuple-element.5, f32[1152]{0:T(1024)S(1)} %get-tuple-element.6, f32[8,1024,16]{1,2,0:T(8,128)S(1)} %copy-done.1, f32[8,1024,16]{1,2,0:T(8,128)S(1)} %add_multiply_fusion.1, f32[8,1024,16]{1,2,0:T(8,128)S(1)} %add.191, f32[8,1024,16]{1,2,0:T(8,128)S(1)} %collective-permute-done.14, ...), kind=kOutput, calls=%fused_computation.36 | convolution fusion | flops 708313088 | bytes 2704384 | tf_op jit(solution)/shard_map/kbnd,dc->kbnc/dot_general | solution.py:11
  342.6 2.0 collective-permute-start.15
  344.5 6.7 %collective-permute-done.15 = f32[8,1024,16]{1,2,0:T(8,128)S(1)} collective-permute-done((f32[8,1024,16]{1,2,0:T(8,128)S(1)}, f32[8,1024,16]{1,2,0:T(8,128)S(1)}, u32[]{:S(2)}, u32[]{:S(2)}) %collective-permute-start.15) | collective-permute-done | bytes 524320 | tf_op jit(solution)/shard_map/ppermute | solution.py:28
  351.3 7.4 %collective-permute-start.16 = (f32[8,1024,16]{1,2,0:T(8,128)S(1)}, f32[8,1024,16]{1,2,0:T(8,128)S(1)}, u32[]{:S(2)}, u32[]{:S(2)}) collective-permute-start(f32[8,1024,16]{1,2,0:T(8,128)S(1)} %add_multiply_fusion), channel_id=1, source_target_pairs={{0,1},{1,2},{2,3},{3,4},{4,5},{5,6},{6,7},{7,8},{8,9},{9,10},{10,1... | collective-permute-start | bytes 1572872 | tf_op jit(solution)/shard_map/ppermute | solution.py:36
  358.7 3.3 collective-permute-done.16
  362.0 0.1 add.198
  362.1 7.1 %collective-permute-start.17 = (f32[8,1024,16]{1,2,0:T(8,128)S(1)}, f32[8,1024,16]{1,2,0:T(8,128)S(1)}, u32[]{:S(2)}, u32[]{:S(2)}) collective-permute-start(f32[8,1024,16]{1,2,0:T(8,128)S(1)} %add.198), channel_id=1, source_target_pairs={{0,2},{1,3},{2,4},{3,5},{4,6},{5,7},{6,8},{7,9},{8,10},{9,11},{10,... | collective-permute-start | bytes 1572872 | tf_op jit(solution)/shard_map/ppermute | solution.py:36
  369.2 9.2 %collective-permute-done.17 = f32[8,1024,16]{1,2,0:T(8,128)S(1)} collective-permute-done((f32[8,1024,16]{1,2,0:T(8,128)S(1)}, f32[8,1024,16]{1,2,0:T(8,128)S(1)}, u32[]{:S(2)}, u32[]{:S(2)}) %collective-permute-start.17) | collective-permute-done | bytes 524320 | tf_op jit(solution)/shard_map/ppermute | solution.py:36
  378.4 3.9 collective-permute-start.18
  382.3 21.1 %collective-permute-done.18 = f32[8,1024,16]{1,2,0:T(8,128)S(1)} collective-permute-done((f32[8,1024,16]{1,2,0:T(8,128)S(1)}, f32[8,1024,16]{1,2,0:T(8,128)S(1)}, u32[]{:S(2)}, u32[]{:S(2)}) %collective-permute-start.18) | collective-permute-done | bytes 524320 | tf_op jit(solution)/shard_map/ppermute | solution.py:36
  403.5 7.7 %collective-permute-start.19 = (f32[8,1024,16]{1,2,0:T(8,128)S(1)}, f32[8,1024,16]{1,2,0:T(8,128)S(1)}, u32[]{:S(2)}, u32[]{:S(2)}) collective-permute-start(f32[8,1024,16]{1,2,0:T(8,128)S(1)} %add.200), channel_id=1, source_target_pairs={{0,8},{1,9},{2,10},{3,11},{4,12},{5,13},{6,14},{7,15},{16,24},{17,... | collective-permute-start | bytes 1572872 | tf_op jit(solution)/shard_map/ppermute | solution.py:36
  411.2 22.7 %collective-permute-done.19 = f32[8,1024,16]{1,2,0:T(8,128)S(1)} collective-permute-done((f32[8,1024,16]{1,2,0:T(8,128)S(1)}, f32[8,1024,16]{1,2,0:T(8,128)S(1)}, u32[]{:S(2)}, u32[]{:S(2)}) %collective-permute-start.19) | collective-permute-done | bytes 524320 | tf_op jit(solution)/shard_map/ppermute | solution.py:36
  433.8 1.0 add_bitcast_fusion
  (20 shorter events, 0.9 us)
Async XLA Ops:
  0.0 0.8 copy-start
  18.2 8.6 %collective-permute-start = (f32[8,1024,16]{1,2,0:T(8,128)S(1)}, f32[8,1024,16]{1,2,0:T(8,128)S(1)}, u32[]{:S(2)}, u32[]{:S(2)}) collective-permute-start(f32[8,1024,16]{1,2,0:T(8,128)S(1)} %fusion.35), channel_id=1, source_target_pairs={{1,0},{2,1},{3,2},{4,3},{5,4},{6,5},{7,6},{8,7},{9,8},{10,9},{11,1... | collective-permute-start | bytes 1572872 | tf_op jit(solution)/shard_map/ppermute | solution.py:28
  26.9 10.7 %collective-permute-start.1 = (f32[8,1024,16]{1,2,0:T(8,128)S(1)}, f32[8,1024,16]{1,2,0:T(8,128)S(1)}, u32[]{:S(2)}, u32[]{:S(2)}) collective-permute-start(f32[8,1024,16]{1,2,0:T(8,128)S(1)} %add_multiply_fusion.3), channel_id=1, source_target_pairs={{0,1},{1,2},{2,3},{3,4},{4,5},{5,6},{6,7},{7,8},{8,9},{9,10},{10,1... | collective-permute-start | bytes 1572872 | tf_op jit(solution)/shard_map/ppermute | solution.py:36
  37.7 15.5 %collective-permute-start.2 = (f32[8,1024,16]{1,2,0:T(8,128)S(1)}, f32[8,1024,16]{1,2,0:T(8,128)S(1)}, u32[]{:S(2)}, u32[]{:S(2)}) collective-permute-start(f32[8,1024,16]{1,2,0:T(8,128)S(1)} %add.171), channel_id=1, source_target_pairs={{0,2},{1,3},{2,4},{3,5},{4,6},{5,7},{6,8},{7,9},{8,10},{9,11},{10,... | collective-permute-start | bytes 1572872 | tf_op jit(solution)/shard_map/ppermute | solution.py:36
  53.2 68.4 %copy-start.1 = (f32[8,1024,16]{1,2,0:T(8,128)S(1)}, f32[8,1024,16]{1,2,0:T(8,128)}, u32[]{:S(2)}) copy-start(f32[8,1024,16]{1,2,0:T(8,128)} %param.6) | copy-start | bytes 1572868
  53.2 68.4 %copy-start.2 = (bf16[16,1152]{1,0:T(8,128)(2,1)S(1)}, bf16[16,1152]{1,0:T(8,128)(2,1)}, u32[]{:S(2)}) copy-start(bf16[16,1152]{1,0:T(8,128)(2,1)} %param.7) | copy-start | bytes 110596
  53.3 40.8 %collective-permute-start.3 = (f32[8,1024,16]{1,2,0:T(8,128)S(1)}, f32[8,1024,16]{1,2,0:T(8,128)S(1)}, u32[]{:S(2)}, u32[]{:S(2)}) collective-permute-start(f32[8,1024,16]{1,2,0:T(8,128)S(1)} %add.172), channel_id=1, source_target_pairs={{0,4},{1,5},{2,6},{3,7},{4,8},{5,9},{6,10},{7,11},{8,12},{9,13},{1... | collective-permute-start | bytes 1572872 | tf_op jit(solution)/shard_map/ppermute | solution.py:36
  94.1 27.6 %collective-permute-start.4 = (f32[8,1024,16]{1,2,0:T(8,128)S(1)}, f32[8,1024,16]{1,2,0:T(8,128)S(1)}, u32[]{:S(2)}, u32[]{:S(2)}) collective-permute-start(f32[8,1024,16]{1,2,0:T(8,128)S(1)} %add.173), channel_id=1, source_target_pairs={{0,8},{1,9},{2,10},{3,11},{4,12},{5,13},{6,14},{7,15},{16,24},{17,... | collective-permute-start | bytes 1572872 | tf_op jit(solution)/shard_map/ppermute | solution.py:36
  138.1 8.6 %collective-permute-start.5 = (f32[8,1024,16]{1,2,0:T(8,128)S(1)}, f32[8,1024,16]{1,2,0:T(8,128)S(1)}, u32[]{:S(2)}, u32[]{:S(2)}) collective-permute-start(f32[8,1024,16]{1,2,0:T(8,128)S(1)} %fusion.34), channel_id=1, source_target_pairs={{1,0},{2,1},{3,2},{4,3},{5,4},{6,5},{7,6},{8,7},{9,8},{10,9},{11,1... | collective-permute-start | bytes 1572872 | tf_op jit(solution)/shard_map/ppermute | solution.py:28
  146.8 10.7 %collective-permute-start.6 = (f32[8,1024,16]{1,2,0:T(8,128)S(1)}, f32[8,1024,16]{1,2,0:T(8,128)S(1)}, u32[]{:S(2)}, u32[]{:S(2)}) collective-permute-start(f32[8,1024,16]{1,2,0:T(8,128)S(1)} %add_multiply_fusion.2), channel_id=1, source_target_pairs={{0,1},{1,2},{2,3},{3,4},{4,5},{5,6},{6,7},{7,8},{8,9},{9,10},{10,1... | collective-permute-start | bytes 1572872 | tf_op jit(solution)/shard_map/ppermute | solution.py:36
  157.6 15.1 %collective-permute-start.7 = (f32[8,1024,16]{1,2,0:T(8,128)S(1)}, f32[8,1024,16]{1,2,0:T(8,128)S(1)}, u32[]{:S(2)}, u32[]{:S(2)}) collective-permute-start(f32[8,1024,16]{1,2,0:T(8,128)S(1)} %add.180), channel_id=1, source_target_pairs={{0,2},{1,3},{2,4},{3,5},{4,6},{5,7},{6,8},{7,9},{8,10},{9,11},{10,... | collective-permute-start | bytes 1572872 | tf_op jit(solution)/shard_map/ppermute | solution.py:36
  172.7 22.8 %collective-permute-start.8 = (f32[8,1024,16]{1,2,0:T(8,128)S(1)}, f32[8,1024,16]{1,2,0:T(8,128)S(1)}, u32[]{:S(2)}, u32[]{:S(2)}) collective-permute-start(f32[8,1024,16]{1,2,0:T(8,128)S(1)} %add.181), channel_id=1, source_target_pairs={{0,4},{1,5},{2,6},{3,7},{4,8},{5,9},{6,10},{7,11},{8,12},{9,13},{1... | collective-permute-start | bytes 1572872 | tf_op jit(solution)/shard_map/ppermute | solution.py:36
  195.6 30.2 %collective-permute-start.9 = (f32[8,1024,16]{1,2,0:T(8,128)S(1)}, f32[8,1024,16]{1,2,0:T(8,128)S(1)}, u32[]{:S(2)}, u32[]{:S(2)}) collective-permute-start(f32[8,1024,16]{1,2,0:T(8,128)S(1)} %add.182), channel_id=1, source_target_pairs={{0,8},{1,9},{2,10},{3,11},{4,12},{5,13},{6,14},{7,15},{16,24},{17,... | collective-permute-start | bytes 1572872 | tf_op jit(solution)/shard_map/ppermute | solution.py:36
  242.3 8.6 %collective-permute-start.10 = (f32[8,1024,16]{1,2,0:T(8,128)S(1)}, f32[8,1024,16]{1,2,0:T(8,128)S(1)}, u32[]{:S(2)}, u32[]{:S(2)}) collective-permute-start(f32[8,1024,16]{1,2,0:T(8,128)S(1)} %fusion.33), channel_id=1, source_target_pairs={{1,0},{2,1},{3,2},{4,3},{5,4},{6,5},{7,6},{8,7},{9,8},{10,9},{11,1... | collective-permute-start | bytes 1572872 | tf_op jit(solution)/shard_map/ppermute | solution.py:28
  251.0 10.7 %collective-permute-start.11 = (f32[8,1024,16]{1,2,0:T(8,128)S(1)}, f32[8,1024,16]{1,2,0:T(8,128)S(1)}, u32[]{:S(2)}, u32[]{:S(2)}) collective-permute-start(f32[8,1024,16]{1,2,0:T(8,128)S(1)} %add_multiply_fusion.1), channel_id=1, source_target_pairs={{0,1},{1,2},{2,3},{3,4},{4,5},{5,6},{6,7},{7,8},{8,9},{9,10},{10,1... | collective-permute-start | bytes 1572872 | tf_op jit(solution)/shard_map/ppermute | solution.py:36
  261.8 14.0 %collective-permute-start.12 = (f32[8,1024,16]{1,2,0:T(8,128)S(1)}, f32[8,1024,16]{1,2,0:T(8,128)S(1)}, u32[]{:S(2)}, u32[]{:S(2)}) collective-permute-start(f32[8,1024,16]{1,2,0:T(8,128)S(1)} %add.189), channel_id=1, source_target_pairs={{0,2},{1,3},{2,4},{3,5},{4,6},{5,7},{6,8},{7,9},{8,10},{9,11},{10,... | collective-permute-start | bytes 1572872 | tf_op jit(solution)/shard_map/ppermute | solution.py:36
  275.8 22.8 %collective-permute-start.13 = (f32[8,1024,16]{1,2,0:T(8,128)S(1)}, f32[8,1024,16]{1,2,0:T(8,128)S(1)}, u32[]{:S(2)}, u32[]{:S(2)}) collective-permute-start(f32[8,1024,16]{1,2,0:T(8,128)S(1)} %add.190), channel_id=1, source_target_pairs={{0,4},{1,5},{2,6},{3,7},{4,8},{5,9},{6,10},{7,11},{8,12},{9,13},{1... | collective-permute-start | bytes 1572872 | tf_op jit(solution)/shard_map/ppermute | solution.py:36
  298.7 27.4 %collective-permute-start.14 = (f32[8,1024,16]{1,2,0:T(8,128)S(1)}, f32[8,1024,16]{1,2,0:T(8,128)S(1)}, u32[]{:S(2)}, u32[]{:S(2)}) collective-permute-start(f32[8,1024,16]{1,2,0:T(8,128)S(1)} %add.191), channel_id=1, source_target_pairs={{0,8},{1,9},{2,10},{3,11},{4,12},{5,13},{6,14},{7,15},{16,24},{17,... | collective-permute-start | bytes 1572872 | tf_op jit(solution)/shard_map/ppermute | solution.py:36
  342.6 8.6 %collective-permute-start.15 = (f32[8,1024,16]{1,2,0:T(8,128)S(1)}, f32[8,1024,16]{1,2,0:T(8,128)S(1)}, u32[]{:S(2)}, u32[]{:S(2)}) collective-permute-start(f32[8,1024,16]{1,2,0:T(8,128)S(1)} %fusion.32), channel_id=1, source_target_pairs={{1,0},{2,1},{3,2},{4,3},{5,4},{6,5},{7,6},{8,7},{9,8},{10,9},{11,1... | collective-permute-start | bytes 1572872 | tf_op jit(solution)/shard_map/ppermute | solution.py:28
  351.3 10.7 %collective-permute-start.16 = (f32[8,1024,16]{1,2,0:T(8,128)S(1)}, f32[8,1024,16]{1,2,0:T(8,128)S(1)}, u32[]{:S(2)}, u32[]{:S(2)}) collective-permute-start(f32[8,1024,16]{1,2,0:T(8,128)S(1)} %add_multiply_fusion), channel_id=1, source_target_pairs={{0,1},{1,2},{2,3},{3,4},{4,5},{5,6},{6,7},{7,8},{8,9},{9,10},{10,1... | collective-permute-start | bytes 1572872 | tf_op jit(solution)/shard_map/ppermute | solution.py:36
  362.1 16.3 %collective-permute-start.17 = (f32[8,1024,16]{1,2,0:T(8,128)S(1)}, f32[8,1024,16]{1,2,0:T(8,128)S(1)}, u32[]{:S(2)}, u32[]{:S(2)}) collective-permute-start(f32[8,1024,16]{1,2,0:T(8,128)S(1)} %add.198), channel_id=1, source_target_pairs={{0,2},{1,3},{2,4},{3,5},{4,6},{5,7},{6,8},{7,9},{8,10},{9,11},{10,... | collective-permute-start | bytes 1572872 | tf_op jit(solution)/shard_map/ppermute | solution.py:36
  378.4 25.0 %collective-permute-start.18 = (f32[8,1024,16]{1,2,0:T(8,128)S(1)}, f32[8,1024,16]{1,2,0:T(8,128)S(1)}, u32[]{:S(2)}, u32[]{:S(2)}) collective-permute-start(f32[8,1024,16]{1,2,0:T(8,128)S(1)} %add.199), channel_id=1, source_target_pairs={{0,4},{1,5},{2,6},{3,7},{4,8},{5,9},{6,10},{7,11},{8,12},{9,13},{1... | collective-permute-start | bytes 1572872 | tf_op jit(solution)/shard_map/ppermute | solution.py:36
  403.5 30.4 %collective-permute-start.19 = (f32[8,1024,16]{1,2,0:T(8,128)S(1)}, f32[8,1024,16]{1,2,0:T(8,128)S(1)}, u32[]{:S(2)}, u32[]{:S(2)}) collective-permute-start(f32[8,1024,16]{1,2,0:T(8,128)S(1)} %add.200), channel_id=1, source_target_pairs={{0,8},{1,9},{2,10},{3,11},{4,12},{5,13},{6,14},{7,15},{16,24},{17,... | collective-permute-start | bytes 1572872 | tf_op jit(solution)/shard_map/ppermute | solution.py:36
where the time goes:
time: 442 us; the launch traced here: 435 us
  waiting for transfers between devices  278 us (63%)
  starting transfers between devices  86.5 us (20%)
  matrix products  66.8 us (15%)
    ppermute x16, waiting for transfers between devices, local(): lax.ppermute(inclusive, 'time', [(source, source + distance) for source i...  252 us
    ppermute x16, starting transfers between devices, local(): lax.ppermute(inclusive, 'time', [(source, source + distance) for source i...  78.6 us
    dot_general x4, matrix products, drift_block(): jnp.einsum('kbnd,dc->kbnc', hidden_act.astype(jnp.bfloat16), w_out, prefe...  66.8 us
    ppermute x4, waiting for transfers between devices, local(): next_first = lax.ppermute(drifts[0], 'time', from_next)  26 us
  transfers between devices with their start and end apart: 20, of which 20 were waited for; matrix products, arithmetic and copies ran while one was open for 0% of the time, Pallas kernels for 0%

commit v1 on v0

v1 whole, which is shorter than its diff:
```python
import functools

import jax
import jax.numpy as jnp
from jax import lax
from jax.experimental import pallas as pl
from jax.experimental.pallas import tpu as pltpu
from jax.sharding import PartitionSpec as P

SWEEPS = 4
TANH_LIN = 0.7978845608028654
TANH_CUB = TANH_LIN * 0.044715
CHUNK = 256
BLOCK = 384
LEAD = 1
LAG = 1


def half_gelu_arg(half):
    square = half * half
    poly = square * (8.0 * TANH_CUB) + 2.0 * TANH_LIN
    gate = jnp.tanh(half * poly)
    return (half * (1.0 + gate)).astype(jnp.bfloat16)


def kernel_body(n_time, x_ref, w_in_ref, w_out_ref, scale_ref, shift_ref, step_ref, out_ref,
                scale_all, shift_all, step_all, weights, x_mine, x_half, d_first, x_out,
                local_sem, mod_send, mod_recv, out_send, out_recv):
    me = lax.axis_index("time")
    channels, hidden = w_in_ref.shape
    batch, _, tokens = x_ref.shape
    mine = batch * tokens // n_time
    per_row = tokens // mine
    n_chunks = mine // CHUNK

    def spot(device):
        return lax.div(device, per_row), lax.rem(device, per_row) * mine

    my_row, my_off = spot(me)
    fetch = pltpu.make_async_copy(x_ref.at[my_row, :, pl.ds(pl.multiple_of(my_off, mine), mine)], x_mine, local_sem.at[0])
    fetch.start()

    barrier = pltpu.get_barrier_semaphore()
    for dist in range(1, n_time):
        pl.semaphore_signal(barrier, inc=1, device_id={"time": lax.rem(me + dist, n_time)}, device_id_type=pl.DeviceIdType.MESH)

    step_all[me] = jnp.full(step_all.shape[1:], step_ref[0], jnp.float32)
    scale_all[me] = scale_ref[...]
    shift_all[me] = shift_ref[...]
    pl.semaphore_wait(barrier, n_time - 1)

    def mod_copies(source, target, slot):
        return [
            pltpu.make_async_remote_copy(src_ref=src, dst_ref=dst.at[source], send_sem=mod_send.at[kind, slot], recv_sem=mod_recv.at[kind, source],
                                         device_id={"time": target}, device_id_type=pl.DeviceIdType.MESH)
            for kind, (src, dst) in enumerate(((scale_ref, scale_all), (shift_ref, shift_all), (step_all.at[me], step_all)))
        ]

    for dist in range(1, n_time):
        for copy in mod_copies(me, lax.rem(me + dist, n_time), dist):
            copy.start()
    fetch.wait()

    @pl.when(me == 0)
    def _():
        whole = pltpu.make_async_copy(x_ref, out_ref, local_sem.at[1])
        whole.start()
        whole.wait()

    for dist in range(1, n_time):
        source = lax.rem(me + dist, n_time)
        for copy in mod_copies(source, source, dist):
            copy.wait_recv()

    w_wide = w_in_ref[...].astype(jnp.float32)

    def prepare(step, carry):
        folded = w_wide * (0.5 * (1.0 + scale_all[step].astype(jnp.float32)))
        high = folded.astype(jnp.bfloat16).astype(jnp.float32)
        rest = folded - high
        middle = rest.astype(jnp.bfloat16).astype(jnp.float32)
        low = rest - middle
        first_row = lax.broadcasted_iota(jnp.int32, (channels, hidden), 0) == 0
        bias = jnp.where(first_row, jnp.broadcast_to(0.5 * shift_all[step].astype(jnp.float32), (channels, hidden)), 0.0)
        stack = jnp.concatenate([high, middle, low, bias], axis=0)
        weights[step] = stack.T.astype(jnp.bfloat16)
        return carry

    lax.fori_loop(0, n_time, prepare, 0)

    ones = jnp.ones((channels, CHUNK), jnp.bfloat16)
    n_blocks = hidden // BLOCK

    def evaluate(steps, get_x, put):
        blocks = [(step, block) for step in steps for block in range(n_blocks)]
        stacked, pre, act, drift = {}, {}, {}, {}

        def project(index):
            step, block = blocks[index]
            if step not in stacked:
                x = get_x(step)
                stacked[step] = jnp.concatenate([x, x, x, ones], axis=0)
            pre[index] = jnp.dot(weights[step, block * BLOCK:(block + 1) * BLOCK, :], stacked[step], preferred_element_type=jnp.float32)

        def contract(index):
            step, block = blocks[index]
            part = jnp.dot(w_out_ref[:, block * BLOCK:(block + 1) * BLOCK], act.pop(index), preferred_element_type=jnp.float32)
            drift[step] = part if block == 0 else drift[step] + part
            if block == n_blocks - 1:
                put(step, drift.pop(step))

        for index in range(len(blocks) + LEAD + LAG):
            if index < len(blocks):
                project(index)
            if LEAD <= index < len(blocks) + LEAD:
                act[index - LEAD] = half_gelu_arg(pre.pop(index - LEAD))
            if index >= LEAD + LAG:
                contract(index - LEAD - LAG)

    def out_copy(chunk, source, target):
        row, off = spot(source)
        cols = pl.ds(pl.multiple_of(off + chunk * CHUNK, CHUNK), CHUNK)
        return pltpu.make_async_remote_copy(
            src_ref=x_out.at[chunk, target], dst_ref=out_ref.at[row, :, cols], send_sem=out_send.at[chunk, target],
            recv_sem=out_recv.at[chunk, source], device_id={"time": target}, device_id_type=pl.DeviceIdType.MESH)

    def run_chunk(chunk, carry):
        start = x_mine[:, pl.ds(pl.multiple_of(chunk * CHUNK, CHUNK), CHUNK)]
        start_half = start.astype(jnp.bfloat16)
        for step in range(1, n_time):
            x_half[step] = start_half

        def put_first(step, drift):
            d_first[...] = drift

        evaluate([0], lambda step: start_half, put_first)

        def sweep(index, carry):
            state = {"last": d_first[...], "x": start}

            def put(step, drift):
                state["x"] = state["x"] + step_all[step - 1] * (0.5 * (state["last"] + drift))
                state["last"] = drift
                x_half[step] = state["x"].astype(jnp.bfloat16)
                x_out[chunk, step] = state["x"]

            evaluate(list(range(1, n_time)), lambda step: x_half[step], put)
            return carry

        lax.fori_loop(0, SWEEPS, sweep, 0)
        for target in range(1, n_time):
            @pl.when(me != target)
            def _():
                out_copy(chunk, me, target).start()

            @pl.when(me == target)
            def _():
                out_ref[my_row, :, pl.ds(pl.multiple_of(my_off + chunk * CHUNK, CHUNK), CHUNK)] = x_out[chunk, target]
        return carry

    lax.fori_loop(0, n_chunks, run_chunk, 0)

    for dist in range(1, n_time):
        for copy in mod_copies(me, lax.rem(me + dist, n_time), dist):
            copy.wait_send()
    for chunk in range(n_chunks):
        for target in range(1, n_time):
            @pl.when(me != target)
            def _():
                out_copy(chunk, me, target).wait_send()

    @pl.when(me != 0)
    def _():
        for chunk in range(n_chunks):
            for dist in range(1, n_time):
                out_copy(chunk, lax.rem(me + dist, n_time), me).wait_recv()


def solution(mesh):
    n_time = mesh.shape["time"]

    def local(x_init, w_in, w_out, mod_scale, mod_shift, step_size):
        batch, tokens, channels = x_init.shape
        hidden = w_in.shape[1]
        mine = batch * tokens // n_time
        n_chunks = mine // CHUNK
        vmem = pl.BlockSpec(memory_space=pltpu.VMEM)
        out = pl.pallas_call(
            functools.partial(kernel_body, n_time),
            out_shape=jax.ShapeDtypeStruct((batch, channels, tokens), jnp.float32),
            in_specs=[pl.BlockSpec(memory_space=pl.ANY), vmem, vmem, vmem, vmem, pl.BlockSpec(memory_space=pltpu.SMEM)],
            out_specs=vmem,
            scratch_shapes=[
                pltpu.VMEM((n_time, 1, hidden), jnp.bfloat16),
                pltpu.VMEM((n_time, 1, hidden), jnp.bfloat16),
                pltpu.VMEM((n_time, 1, CHUNK), jnp.float32),
                pltpu.VMEM((n_time, hidden, 4 * channels), jnp.bfloat16),
                pltpu.VMEM((channels, mine), jnp.float32),
                pltpu.VMEM((n_time, channels, CHUNK), jnp.bfloat16),
                pltpu.VMEM((channels, CHUNK), jnp.float32),
                pltpu.VMEM((n_chunks, n_time, channels, CHUNK), jnp.float32),
                pltpu.SemaphoreType.DMA((2,)),
                pltpu.SemaphoreType.DMA((3, n_time)),
                pltpu.SemaphoreType.DMA((3, n_time)),
                pltpu.SemaphoreType.DMA((n_chunks, n_time)),
                pltpu.SemaphoreType.DMA((n_chunks, n_time)),
            ],
            compiler_params=pltpu.CompilerParams(collective_id=0, has_side_effects=True, vmem_limit_bytes=48 * 2**20),
            name="picard",
        )(jnp.swapaxes(x_init, 1, 2), w_in, w_out.T, mod_scale, mod_shift, step_size)
        return jnp.swapaxes(out, 1, 2)[None]

    return jax.shard_map(local, mesh=mesh, in_specs=(P("data"), P(), P(), P("time"), P("time"), P("time")), out_specs=P("time", "data"), check_vma=False)
```

time: 442 us -> 70.4 us (0.16)
  the two profiles are of different devices: /device:TPU:54 before, /device:TPU:21 now
where the time goes in v1:
time: 70.4 us; the launch traced here: 70.1 us
  Pallas kernels  65.3 us (93%)
  local copies, waits for them, and re-layouts  4.08 us (6%)
    pallas_call x1, Pallas kernels, local(): pl.pallas_call(functools.partial(kernel_body, n_time), out_shape=jax.Shap...  65.3 us
    unnamed x11, local copies, waits for them, and re-layouts  4.08 us

profile of v1, /device:TPU:21, one launch (start us, length us, event | category | flops | bytes accessed | tf_op | source)
XLA Modules:
  0.0 70.1 jit_solution(7842131463530370757)
XLA Ops:
  0.0 0.0 copy-start.3
  0.7 0.0 copy-done.3
  0.7 0.0 copy-start
  0.7 1.0 %copy-done = f32[8,1024,16]{1,2,0:T(8,128)S(1)} copy-done((f32[8,1024,16]{1,2,0:T(8,128)S(1)}, f32[8,1024,16]{1,2,0:T(8,128)}, u32[]{:S(2)}) %copy-start) | copy-done | bytes 524312
  1.7 0.0 copy-start.1
  1.7 0.8 %copy-done.1 = bf16[16,1152]{1,0:T(8,128)(2,1)S(1)} copy-done((bf16[16,1152]{1,0:T(8,128)(2,1)S(1)}, bf16[16,1152]{1,0:T(8,128)(2,1)}, u32[]{:S(2)}) %copy-start.1) | copy-done | bytes 36888
  2.5 0.0 copy-start.2
  2.5 0.8 %copy-done.2 = bf16[1152,16]{0,1:T(8,128)(2,1)S(1)} copy-done((bf16[1152,16]{0,1:T(8,128)(2,1)S(1)}, bf16[1152,16]{0,1:T(8,128)(2,1)}, u32[]{:S(2)}) %copy-start.2) | copy-done | bytes 36888
  3.3 0.0 copy-start.4
  3.3 0.7 copy-done.4
  4.0 65.3 %picard.1 = f32[8,16,1024]{2,1,0:T(8,128)S(1)} custom-call(f32[8,16,1024]{2,1,0:T(8,128)S(1)} %bitcast.6, bf16[16,1152]{1,0:T(8,128)(2,1)S(1)} %copy-done.1, bf16[16,1152]{1,0:T(8,128)(2,1)S(1)} %bitcast.7, bf16[1,1152]{1,0:T(2,128)(2,1)S(1)} %copy-done.3, bf16[1,1152]{1,0:T(2,128)(2,1)S(1)} %copy-done.4, f32[1]{0:T(128)S(6)} %copy.8.step_ref), custom_call_target="tpu_custom_call" | custom-call | tf_op jit(solution)/shard_map/picard/pallas_call | solution.py:188
  69.3 0.8 %copy.9 = f32[1,8,1024,16]{2,3,1,0:T(8,128)} copy(f32[1,8,1024,16]{2,3,1,0:T(8,128)S(1)} %bitcast.5) | data formatting | bytes 1048576
Async XLA Ops:
  0.0 0.7 copy-start.3
  0.7 1.0 %copy-start = (f32[8,1024,16]{1,2,0:T(8,128)S(1)}, f32[8,1024,16]{1,2,0:T(8,128)}, u32[]{:S(2)}) copy-start(f32[8,1024,16]{1,2,0:T(8,128)} %param.6) | copy-start | bytes 1572868
  1.7 0.8 %copy-start.1 = (bf16[16,1152]{1,0:T(8,128)(2,1)S(1)}, bf16[16,1152]{1,0:T(8,128)(2,1)}, u32[]{:S(2)}) copy-start(bf16[16,1152]{1,0:T(8,128)(2,1)} %w_in_ref.1) | copy-start | bytes 110596
  2.5 0.8 %copy-start.2 = (bf16[1152,16]{0,1:T(8,128)(2,1)S(1)}, bf16[1152,16]{0,1:T(8,128)(2,1)}, u32[]{:S(2)}) copy-start(bf16[1152,16]{0,1:T(8,128)(2,1)} %param.8) | copy-start | bytes 110596
  3.3 0.7 copy-start.4

commit v2 on v1

v2 whole, which is shorter than its diff:
```python
import functools

import jax
import jax.numpy as jnp
from jax import lax
from jax.experimental import pallas as pl
from jax.experimental.pallas import tpu as pltpu
from jax.sharding import PartitionSpec as P

SWEEPS = 4
TANH_LIN = 0.7978845608028654
TANH_CUB = TANH_LIN * 0.044715
CHUNK = 256
BLOCK = 384
LEAD = 1
LAG = 1
SEND_AFTER = (8, 13)


def half_gelu_arg(half):
    square = half * half
    poly = square * (8.0 * TANH_CUB) + 2.0 * TANH_LIN
    gate = jnp.tanh(half * poly)
    return (half * (1.0 + gate)).astype(jnp.bfloat16)


def kernel_body(n_time, x_ref, w_in_ref, w_out_ref, scale_ref, shift_ref, step_ref, out_ref,
                w_in, w_out, step_own, scale_all, shift_all, step_all, weights, x_mine, x_half, drifts, x_out,
                local_sem, whole_sem, mod_send, mod_recv, out_send, out_recv):
    me = lax.axis_index("time")
    channels, hidden = w_in.shape
    batch, _, tokens = x_ref.shape
    mine = batch * tokens // n_time
    per_row = tokens // mine
    n_chunks = mine // CHUNK
    n_blocks = hidden // BLOCK
    n_chips = n_time // 2

    def spot(device):
        return lax.div(device, per_row), lax.rem(device, per_row) * mine

    my_row, my_off = spot(me)
    fetches = [
        pltpu.make_async_copy(src, dst, local_sem.at[slot])
        for slot, (src, dst) in enumerate((
            (scale_ref, scale_all.at[me]), (shift_ref, shift_all.at[me]), (step_ref, step_own), (w_in_ref, w_in), (w_out_ref, w_out),
            (x_ref.at[my_row, :, pl.ds(pl.multiple_of(my_off, mine), mine)], x_mine)))
    ]
    for fetch in fetches:
        fetch.start()

    chip, core = lax.div(me, 2), lax.rem(me, 2)

    def peer_of(slot):
        return lax.rem(chip + slot // 2, n_chips) * 2 + lax.rem(core + slot % 2, 2)

    def slot_of(step):
        return lax.rem(step // 2 + n_chips - chip, n_chips) * 2 + lax.rem(step % 2 + 2 - core, 2)

    groups = [[1]]
    for dist in range(1, n_chips // 2 + 1):
        ways = (dist,) if 2 * dist == n_chips else (dist, n_chips - dist)
        groups.append([way * 2 + other for way in ways for other in range(2)])
    near_first = [slot for group in groups for slot in group]

    barrier = pltpu.get_barrier_semaphore()
    for slot in reversed(near_first):
        pl.semaphore_signal(barrier, inc=1, device_id={"time": peer_of(slot)}, device_id_type=pl.DeviceIdType.MESH)
    for fetch in fetches:
        fetch.wait()
    step_all[me] = jnp.full(step_all.shape[1:], step_own[0], jnp.float32)

    @pl.when(me == 0)
    def _():
        pltpu.make_async_copy(x_ref, out_ref, whole_sem.at[0]).start()

    def mod_copies(source, target, slot):
        return [
            pltpu.make_async_remote_copy(src_ref=ref.at[source], dst_ref=ref.at[source], send_sem=mod_send.at[kind, slot], recv_sem=mod_recv.at[kind, source],
                                         device_id={"time": target}, device_id_type=pl.DeviceIdType.MESH)
            for kind, ref in enumerate((scale_all, shift_all, step_all))
        ]

    def prepare(slot):
        step = peer_of(slot)
        folded = w_in[...].astype(jnp.float32) * (0.5 * (1.0 + scale_all[step].astype(jnp.float32)))
        high = folded.astype(jnp.bfloat16).astype(jnp.float32)
        rest = folded - high
        middle = rest.astype(jnp.bfloat16).astype(jnp.float32)
        low = rest - middle
        first_row = lax.broadcasted_iota(jnp.int32, (channels, hidden), 0) == 0
        bias = jnp.where(first_row, jnp.broadcast_to(0.5 * shift_all[step].astype(jnp.float32), (channels, hidden)), 0.0)
        stack = jnp.concatenate([high, middle, low, bias], axis=0)
        weights[slot] = stack.T.astype(jnp.bfloat16)

    ones = jnp.ones((channels, CHUNK), jnp.bfloat16)

    def evaluate(items, extras=()):
        extras = list(extras)
        blocks = [(item, block) for item in range(len(items)) for block in range(n_blocks)]
        every = max(1, len(blocks) // max(1, len(extras)))
        stacked, pre, act, drift = {}, {}, {}, {}

        def project(index):
            item, block = blocks[index]
            slot, get_x, _ = items[item]
            if item not in stacked:
                x = get_x()
                stacked[item] = jnp.concatenate([x, x, x, ones], axis=0)
            pre[index] = jnp.dot(weights[slot, block * BLOCK:(block + 1) * BLOCK, :], stacked[item], preferred_element_type=jnp.float32)

        def contract(index):
            item, block = blocks[index]
            part = jnp.dot(w_out[:, block * BLOCK:(block + 1) * BLOCK], act.pop(index), preferred_element_type=jnp.float32)
            drift[item] = part if block == 0 else drift[item] + part
            if block == n_blocks - 1:
                items[item][2](drift.pop(item))

        for index in range(len(blocks) + LEAD + LAG):
            if index < len(blocks):
                project(index)
                if extras and index % every == 0:
                    extras.pop(0)()
            if LEAD <= index < len(blocks) + LEAD:
                act[index - LEAD] = half_gelu_arg(pre.pop(index - LEAD))
            if index >= LEAD + LAG:
                contract(index - LEAD - LAG)
        for extra in extras:
            extra()

    def columns(chunk):
        return pl.ds(pl.multiple_of(chunk * CHUNK, CHUNK), CHUNK)

    def first_items(slots):
        def item(slot, chunk):
            def put(drift):
                drifts[slot, chunk] = drift
            return slot, lambda: x_mine[:, columns(chunk)].astype(jnp.bfloat16), put
        return [item(slot, chunk) for slot in slots for chunk in range(n_chunks)]

    prepare(0)
    pl.semaphore_wait(barrier, n_time - 1)
    for slot in near_first:
        for copy in mod_copies(me, peer_of(slot), slot):
            copy.start()

    evaluate(first_items([0]))
    ready = []
    for arrival in (groups[0] + groups[1], groups[2], [slot for group in groups[3:] for slot in group]):
        for slot in arrival:
            for copy in mod_copies(peer_of(slot), peer_of(slot), slot):
                copy.wait_recv()
        evaluate(first_items(ready), [functools.partial(prepare, slot) for slot in arrival])
        ready = arrival
    evaluate(first_items(ready))

    def integrate(chunk):
        last, x = drifts[slot_of(0), chunk], x_mine[:, columns(chunk)]
        for step in range(1, n_time):
            drift = drifts[slot_of(step), chunk]
            x = x + step_all[step - 1] * (0.5 * (last + drift))
            last = drift
            x_half[step] = x.astype(jnp.bfloat16)

    def out_copy(chunk, source, target):
        row, off = spot(source)
        cols = pl.ds(pl.multiple_of(off + chunk * CHUNK, CHUNK), CHUNK)
        return pltpu.make_async_remote_copy(
            src_ref=x_out.at[chunk, target], dst_ref=out_ref.at[row, :, cols], send_sem=out_send.at[chunk, target],
            recv_sem=out_recv.at[chunk, source], device_id={"time": target}, device_id_type=pl.DeviceIdType.MESH)

    def sweep_items(chunk, steps, state, keep):
        def item(step):
            def put(drift):
                state["x"] = state["x"] + step_all[step - 1] * (0.5 * (state["last"] + drift))
                state["last"] = drift
                if keep:
                    x_out[chunk, step] = state["x"]
                else:
                    x_half[step] = state["x"].astype(jnp.bfloat16)
            return slot_of(step), lambda: x_half[step], put
        return [item(step) for step in steps]

    def run_chunk(chunk, carry):
        integrate(chunk)

        def sweep(index, carry):
            state = {"last": drifts[slot_of(0), chunk], "x": x_mine[:, columns(chunk)]}
            evaluate(sweep_items(chunk, range(1, n_time), state, False))
            return carry

        lax.fori_loop(1, SWEEPS - 1, sweep, 0)
        state = {"last": drifts[slot_of(0), chunk], "x": x_mine[:, columns(chunk)]}
        begin = 1
        for end in SEND_AFTER + (n_time,):
            evaluate(sweep_items(chunk, range(begin, end), state, True))
            for target in range(begin, end):
                @pl.when(me != target)
                def _():
                    out_copy(chunk, me, target).start()
            begin = end

        @pl.when(me != 0)
        def _():
            out_ref[my_row, :, pl.ds(pl.multiple_of(my_off + chunk * CHUNK, CHUNK), CHUNK)] = x_out[chunk, me]
        return carry

    lax.fori_loop(0, n_chunks, run_chunk, 0)

    for slot in near_first:
        for copy in mod_copies(me, peer_of(slot), slot):
            copy.wait_send()

    @pl.when(me == 0)
    def _():
        pltpu.make_async_copy(x_ref, out_ref, whole_sem.at[0]).wait()

    for chunk in range(n_chunks):
        for target in range(1, n_time):
            @pl.when(me != target)
            def _():
                out_copy(chunk, me, target).wait_send()

    @pl.when(me != 0)
    def _():
        for chunk in range(n_chunks):
            for dist in range(1, n_time):
                out_copy(chunk, lax.rem(me + dist, n_time), me).wait_recv()


def solution(mesh):
    n_time = mesh.shape["time"]

    def local(x_init, w_in, w_out, mod_scale, mod_shift, step_size):
        batch, tokens, channels = x_init.shape
        hidden = w_in.shape[1]
        mine = batch * tokens // n_time
        n_chunks = mine // CHUNK
        out = pl.pallas_call(
            functools.partial(kernel_body, n_time),
            out_shape=jax.ShapeDtypeStruct((batch, channels, tokens), jnp.float32),
            in_specs=[pl.BlockSpec(memory_space=pltpu.HBM)] * 6,
            out_specs=pl.BlockSpec(memory_space=pltpu.VMEM),
            scratch_shapes=[
                pltpu.VMEM((channels, hidden), jnp.bfloat16),
                pltpu.VMEM((channels, hidden), jnp.bfloat16),
                pltpu.SMEM((1,), jnp.float32),
                pltpu.VMEM((n_time, 1, hidden), jnp.bfloat16),
                pltpu.VMEM((n_time, 1, hidden), jnp.bfloat16),
                pltpu.VMEM((n_time, 1, CHUNK), jnp.float32),
                pltpu.VMEM((n_time, hidden, 4 * channels), jnp.bfloat16),
                pltpu.VMEM((channels, mine), jnp.float32),
                pltpu.VMEM((n_time, channels, CHUNK), jnp.bfloat16),
                pltpu.VMEM((n_time, n_chunks, channels, CHUNK), jnp.float32),
                pltpu.VMEM((n_chunks, n_time, channels, CHUNK), jnp.float32),
                pltpu.SemaphoreType.DMA((6,)),
                pltpu.SemaphoreType.DMA((1,)),
                pltpu.SemaphoreType.DMA((3, n_time)),
                pltpu.SemaphoreType.DMA((3, n_time)),
                pltpu.SemaphoreType.DMA((n_chunks, n_time)),
                pltpu.SemaphoreType.DMA((n_chunks, n_time)),
            ],
            compiler_params=pltpu.CompilerParams(collective_id=0, has_side_effects=True, vmem_limit_bytes=48 * 2**20),
            name="picard",
        )(*(pltpu.with_memory_space_constraint(a, pltpu.HBM) for a in (jnp.swapaxes(x_init, 1, 2), w_in, w_out.T, mod_scale, mod_shift)), step_size)
        return jnp.swapaxes(out, 1, 2)[None]

    return jax.shard_map(local, mesh=mesh, in_specs=(P("data"), P(), P(), P("time"), P("time"), P("time")), out_specs=P("time", "data"), check_vma=False)
```

time: 70.4 us -> 63.2 us (0.90)
  Pallas kernels: 65.3 us -> 61.6 us
  local copies, waits for them, and re-layouts: 4.08 us -> 0.8 us
    pallas_call x1, Pallas kernels: 65.3 us -> 61.6 us  [local(): pl.pallas_call(functools.partial(kernel_body, n_time), out_shape=jax.Shap...]
    unnamed x11 -> x1, local copies, waits for them, and re-layouts: 4.08 us -> 0.8 us
where the time goes in v2:
time: 63.2 us; the launch traced here: 63.1 us
  Pallas kernels  61.6 us (97%)
  local copies, waits for them, and re-layouts  0.8 us (1%)
  between operations  0.66 us (1%)
    pallas_call x1, Pallas kernels, local(): pl.pallas_call(functools.partial(kernel_body, n_time), out_shape=jax.Shap...  61.6 us

profile of v2, /device:TPU:21, one launch (start us, length us, event | category | flops | bytes accessed | tf_op | source)
XLA Modules:
  0.0 63.1 jit_solution(10747351830023153856)
XLA Ops:
  0.7 61.6 %picard.1 = f32[8,16,1024]{2,1,0:T(8,128)S(1)} custom-call(f32[8,16,1024]{2,1,0:T(8,128)} %bitcast.6, bf16[16,1152]{1,0:T(8,128)(2,1)} %w_in_ref.1, bf16[16,1152]{1,0:T(8,128)(2,1)} %bitcast.7, bf16[1,1152]{1,0:T(2,128)(2,1)} %scale_ref.1, bf16[1,1152]{1,0:T(2,128)(2,1)} %shift_ref.1, f32[1]{0:T(128)S(6)} %copy.8.step_ref), custom_call_target="tpu_custom_call" | custom-call | tf_op jit(solution)/shard_map/picard/pallas_call | solution.py:239
  62.3 0.8 %copy.9 = f32[1,8,1024,16]{2,3,1,0:T(8,128)} copy(f32[1,8,1024,16]{2,3,1,0:T(8,128)S(1)} %bitcast.5) | data formatting | bytes 1048576

commit v3 on v2

--- a/solution.py
+++ b/solution.py
@@ -14,7 +14,8 @@
 BLOCK = 384
 LEAD = 1
 LAG = 1
-SEND_AFTER = (8, 13)
+SEND_AFTER = (6, 11, 14)
+WAIT_AT = 1
 
 
 def half_gelu_arg(half):
@@ -25,7 +26,7 @@
 
 
 def kernel_body(n_time, x_ref, w_in_ref, w_out_ref, scale_ref, shift_ref, step_ref, out_ref,
-                w_in, w_out, step_own, scale_all, shift_all, step_all, weights, x_mine, x_half, drifts, x_out,
+                w_in, w_out, step_own, scale_own, shift_own, mods_all, step_all, weights, x_mine, x_half, drifts, x_out,
                 local_sem, whole_sem, mod_send, mod_recv, out_send, out_recv):
     me = lax.axis_index("time")
     channels, hidden = w_in.shape
@@ -43,7 +44,7 @@
     fetches = [
         pltpu.make_async_copy(src, dst, local_sem.at[slot])
         for slot, (src, dst) in enumerate((
-            (scale_ref, scale_all.at[me]), (shift_ref, shift_all.at[me]), (step_ref, step_own), (w_in_ref, w_in), (w_out_ref, w_out),
+            (scale_ref, scale_own), (shift_ref, shift_own), (step_ref, step_own), (w_in_ref, w_in), (w_out_ref, w_out),
             (x_ref.at[my_row, :, pl.ds(pl.multiple_of(my_off, mine), mine)], x_mine)))
     ]
     for fetch in fetches:
@@ -68,6 +69,7 @@
         pl.semaphore_signal(barrier, inc=1, device_id={"time": peer_of(slot)}, device_id_type=pl.DeviceIdType.MESH)
     for fetch in fetches:
         fetch.wait()
+    mods_all[me] = jnp.concatenate([scale_own[...], shift_own[...]], axis=0)
     step_all[me] = jnp.full(step_all.shape[1:], step_own[0], jnp.float32)
 
     @pl.when(me == 0)
@@ -78,27 +80,26 @@
         return [
             pltpu.make_async_remote_copy(src_ref=ref.at[source], dst_ref=ref.at[source], send_sem=mod_send.at[kind, slot], recv_sem=mod_recv.at[kind, source],
                                          device_id={"time": target}, device_id_type=pl.DeviceIdType.MESH)
-            for kind, ref in enumerate((scale_all, shift_all, step_all))
+            for kind, ref in enumerate((mods_all, step_all))
         ]
 
     def prepare(slot):
-        step = peer_of(slot)
-        folded = w_in[...].astype(jnp.float32) * (0.5 * (1.0 + scale_all[step].astype(jnp.float32)))
+        mods = mods_all[peer_of(slot)].astype(jnp.float32)
+        folded = w_in[...].astype(jnp.float32) * (0.5 * (1.0 + mods[0:1]))
         high = folded.astype(jnp.bfloat16).astype(jnp.float32)
         rest = folded - high
         middle = rest.astype(jnp.bfloat16).astype(jnp.float32)
         low = rest - middle
         first_row = lax.broadcasted_iota(jnp.int32, (channels, hidden), 0) == 0
-        bias = jnp.where(first_row, jnp.broadcast_to(0.5 * shift_all[step].astype(jnp.float32), (channels, hidden)), 0.0)
+        bias = jnp.where(first_row, jnp.broadcast_to(0.5 * mods[1:2], (channels, hidden)), 0.0)
         stack = jnp.concatenate([high, middle, low, bias], axis=0)
         weights[slot] = stack.T.astype(jnp.bfloat16)
 
     ones = jnp.ones((channels, CHUNK), jnp.bfloat16)
 
-    def evaluate(items, extras=()):
-        extras = list(extras)
+    def evaluate(items, extras=None):
+        extras = extras or {}
         blocks = [(item, block) for item in range(len(items)) for block in range(n_blocks)]
-        every = max(1, len(blocks) // max(1, len(extras)))
         stacked, pre, act, drift = {}, {}, {}, {}
 
         def project(index):
@@ -118,15 +119,13 @@
 
         for index in range(len(blocks) + LEAD + LAG):
             if index < len(blocks):
+                for extra in extras.get(index, ()):
+                    extra()
                 project(index)
-                if extras and index % every == 0:
-                    extras.pop(0)()
             if LEAD <= index < len(blocks) + LEAD:
                 act[index - LEAD] = half_gelu_arg(pre.pop(index - LEAD))
             if index >= LEAD + LAG:
                 contract(index - LEAD - LAG)
-        for extra in extras:
-            extra()
 
     def columns(chunk):
         return pl.ds(pl.multiple_of(chunk * CHUNK, CHUNK), CHUNK)
@@ -144,15 +143,22 @@
         for copy in mod_copies(me, peer_of(slot), slot):
             copy.start()
 
-    evaluate(first_items([0]))
-    ready = []
-    for arrival in (groups[0] + groups[1], groups[2], [slot for group in groups[3:] for slot in group]):
-        for slot in arrival:
+    def arrive(slots):
+        for slot in slots:
             for copy in mod_copies(peer_of(slot), peer_of(slot), slot):
                 copy.wait_recv()
-        evaluate(first_items(ready), [functools.partial(prepare, slot) for slot in arrival])
-        ready = arrival
-    evaluate(first_items(ready))
+
+    evaluate(first_items([0]))
+    near, middle = len(groups[0] + groups[1]), len(groups[2])
+    arrive(near_first[:near])
+    for slot in near_first[:near]:
+        prepare(slot)
+    per_slot = n_chunks * n_blocks
+    extras = {WAIT_AT * per_slot: [functools.partial(arrive, near_first[near:near + middle])],
+              (WAIT_AT + middle) * per_slot: [functools.partial(arrive, near_first[near + middle:])]}
+    for place, slot in enumerate(near_first[near:]):
+        extras.setdefault((WAIT_AT + place) * per_slot + 1, []).append(functools.partial(prepare, slot))
+    evaluate(first_items(near_first), extras)
 
     def integrate(chunk):
         last, x = drifts[slot_of(0), chunk], x_mine[:, columns(chunk)]
@@ -169,43 +175,53 @@
             src_ref=x_out.at[chunk, target], dst_ref=out_ref.at[row, :, cols], send_sem=out_send.at[chunk, target],
             recv_sem=out_recv.at[chunk, source], device_id={"time": target}, device_id_type=pl.DeviceIdType.MESH)
 
-    def sweep_items(chunk, steps, state, keep):
+    def sweep_items(chunk, steps, state):
         def item(step):
             def put(drift):
                 state["x"] = state["x"] + step_all[step - 1] * (0.5 * (state["last"] + drift))
                 state["last"] = drift
-                if keep:
-                    x_out[chunk, step] = state["x"]
-                else:
-                    x_half[step] = state["x"].astype(jnp.bfloat16)
+                x_half[step] = state["x"].astype(jnp.bfloat16)
+                x_out[chunk, step] = state["x"]
             return slot_of(step), lambda: x_half[step], put
         return [item(step) for step in steps]
 
-    def run_chunk(chunk, carry):
-        integrate(chunk)
-
-        def sweep(index, carry):
-            state = {"last": drifts[slot_of(0), chunk], "x": x_mine[:, columns(chunk)]}
-            evaluate(sweep_items(chunk, range(1, n_time), state, False))
-            return carry
-
-        lax.fori_loop(1, SWEEPS - 1, sweep, 0)
-        state = {"last": drifts[slot_of(0), chunk], "x": x_mine[:, columns(chunk)]}
-        begin = 1
-        for end in SEND_AFTER + (n_time,):
-            evaluate(sweep_items(chunk, range(begin, end), state, True))
-            for target in range(begin, end):
-                @pl.when(me != target)
-                def _():
-                    out_copy(chunk, me, target).start()
-            begin = end
-
+    def initial(chunk):
+        return {"last": drifts[slot_of(0), chunk], "x": x_mine[:, columns(chunk)]}
+
+    def send(chunk, targets):
+        for target in targets:
+            @pl.when(me != target)
+            def _():
+                out_copy(chunk, me, target).start()
+
+    def keep(chunk):
         @pl.when(me != 0)
         def _():
             out_ref[my_row, :, pl.ds(pl.multiple_of(my_off + chunk * CHUNK, CHUNK), CHUNK)] = x_out[chunk, me]
+
+    later = SWEEPS - 1
+
+    def sweep(index, carry):
+        chunk = lax.div(index, later)
+        evaluate(sweep_items(chunk, range(1, n_time), initial(chunk)))
+
+        @pl.when(jnp.logical_and(lax.rem(index, later) == later - 1, chunk < n_chunks - 1))
+        def _():
+            send(chunk, range(1, n_time))
+            keep(chunk)
+            integrate(chunk + 1)
         return carry
 
-    lax.fori_loop(0, n_chunks, run_chunk, 0)
+    integrate(0)
+    lax.fori_loop(0, n_chunks * later - 1, sweep, 0)
+    final = n_chunks - 1
+    state = initial(final)
+    begin = 1
+    for end in SEND_AFTER + (n_time,):
+        evaluate(sweep_items(final, range(begin, end), state))
+        send(final, range(begin, end))
+        begin = end
+    keep(final)
 
     for slot in near_first:
         for copy in mod_copies(me, peer_of(slot), slot):
@@ -245,8 +261,9 @@
                 pltpu.VMEM((channels, hidden), jnp.bfloat16),
                 pltpu.VMEM((channels, hidden), jnp.bfloat16),
                 pltpu.SMEM((1,), jnp.float32),
-                pltpu.VMEM((n_time, 1, hidden), jnp.bfloat16),
-                pltpu.VMEM((n_time, 1, hidden), jnp.bfloat16),
+                pltpu.VMEM((1, hidden), jnp.bfloat16),
+                pltpu.VMEM((1, hidden), jnp.bfloat16),
+                pltpu.VMEM((n_time, 2, hidden), jnp.bfloat16),
                 pltpu.VMEM((n_time, 1, CHUNK), jnp.float32),
                 pltpu.VMEM((n_time, hidden, 4 * channels), jnp.bfloat16),
                 pltpu.VMEM((channels, mine), jnp.float32),
@@ -255,8 +272,8 @@
                 pltpu.VMEM((n_chunks, n_time, channels, CHUNK), jnp.float32),
                 pltpu.SemaphoreType.DMA((6,)),
                 pltpu.SemaphoreType.DMA((1,)),
-                pltpu.SemaphoreType.DMA((3, n_time)),
-                pltpu.SemaphoreType.DMA((3, n_time)),
+                pltpu.SemaphoreType.DMA((2, n_time)),
+                pltpu.SemaphoreType.DMA((2, n_time)),
                 pltpu.SemaphoreType.DMA((n_chunks, n_time)),
                 pltpu.SemaphoreType.DMA((n_chunks, n_time)),
             ],

time: 63.2 us -> 59.6 us (0.943)
  the two profiles are of different devices: /device:TPU:21 before, /device:TPU:22 now
where the time goes in v3:
time: 59.6 us; the launch traced here: 59.4 us
  Pallas kernels  58 us (97%)
  local copies, waits for them, and re-layouts  0.8 us (1%)
  between operations  0.66 us (1%)
    pallas_call x1, Pallas kernels, local(): pl.pallas_call(functools.partial(kernel_body, n_time), out_shape=jax.Shap...  58 us

profile of v3, /device:TPU:22, one launch (start us, length us, event | category | flops | bytes accessed | tf_op | source)
XLA Modules:
  0.0 59.4 jit_solution(6308512838946756289)
XLA Ops:
  0.7 58.0 %picard.1 = f32[8,16,1024]{2,1,0:T(8,128)S(1)} custom-call(f32[8,16,1024]{2,1,0:T(8,128)} %bitcast.6, bf16[16,1152]{1,0:T(8,128)(2,1)} %w_in_ref.1, bf16[16,1152]{1,0:T(8,128)(2,1)} %bitcast.7, bf16[1,1152]{1,0:T(2,128)(2,1)} %scale_ref.1, bf16[1,1152]{1,0:T(2,128)(2,1)} %shift_ref.1, f32[1]{0:T(128)S(6)} %copy.8.step_ref), custom_call_target="tpu_custom_call" | custom-call | tf_op jit(solution)/shard_map/picard/pallas_call | solution.py:255
  58.6 0.8 %copy.9 = f32[1,8,1024,16]{2,3,1,0:T(8,128)} copy(f32[1,8,1024,16]{2,3,1,0:T(8,128)S(1)} %bitcast.5) | data formatting | bytes 1048576

commit v4 on v3

--- a/solution.py
+++ b/solution.py
@@ -14,8 +14,8 @@
 BLOCK = 384
 LEAD = 1
 LAG = 1
-SEND_AFTER = (6, 11, 14)
 WAIT_AT = 1
+SEND_AFTER = (5, 9, 12, 14)
 
 
 def half_gelu_arg(half):
@@ -26,7 +26,7 @@
 
 
 def kernel_body(n_time, x_ref, w_in_ref, w_out_ref, scale_ref, shift_ref, step_ref, out_ref,
-                w_in, w_out, step_own, scale_own, shift_own, mods_all, step_all, weights, x_mine, x_half, drifts, x_out,
+                w_in, w_out, step_own, scale_own, shift_own, mods_all, step_all, weights, x_mine, x_half, drifts, x_out, landed,
                 local_sem, whole_sem, mod_send, mod_recv, out_send, out_recv):
     me = lax.axis_index("time")
     channels, hidden = w_in.shape
@@ -74,7 +74,7 @@
 
     @pl.when(me == 0)
     def _():
-        pltpu.make_async_copy(x_ref, out_ref, whole_sem.at[0]).start()
+        pltpu.make_async_copy(x_ref, landed.at[pl.ds(0, batch)], whole_sem.at[0]).start()
 
     def mod_copies(source, target, slot):
         return [
@@ -117,14 +117,14 @@
             if block == n_blocks - 1:
                 items[item][2](drift.pop(item))
 
-        for index in range(len(blocks) + LEAD + LAG):
+        for index in range(len(blocks) + LEAD + LAG + 1):
+            for extra in extras.get(index, ()):
+                extra()
             if index < len(blocks):
-                for extra in extras.get(index, ()):
-                    extra()
                 project(index)
             if LEAD <= index < len(blocks) + LEAD:
                 act[index - LEAD] = half_gelu_arg(pre.pop(index - LEAD))
-            if index >= LEAD + LAG:
+            if LEAD + LAG <= index < len(blocks) + LEAD + LAG:
                 contract(index - LEAD - LAG)
 
     def columns(chunk):
@@ -171,9 +171,11 @@
     def out_copy(chunk, source, target):
         row, off = spot(source)
         cols = pl.ds(pl.multiple_of(off + chunk * CHUNK, CHUNK), CHUNK)
+        own = source == target
         return pltpu.make_async_remote_copy(
-            src_ref=x_out.at[chunk, target], dst_ref=out_ref.at[row, :, cols], send_sem=out_send.at[chunk, target],
-            recv_sem=out_recv.at[chunk, source], device_id={"time": target}, device_id_type=pl.DeviceIdType.MESH)
+            src_ref=x_out.at[chunk, target], dst_ref=landed.at[jnp.where(own, batch, row), :, cols], send_sem=out_send.at[chunk, target],
+            recv_sem=out_recv.at[chunk, jnp.where(own, n_time, source)], device_id={"time": jnp.where(own, target + 1 - 2 * lax.rem(target, 2), target)},
+            device_id_type=pl.DeviceIdType.MESH)
 
     def sweep_items(chunk, steps, state):
         def item(step):
@@ -188,16 +190,13 @@
     def initial(chunk):
         return {"last": drifts[slot_of(0), chunk], "x": x_mine[:, columns(chunk)]}
 
-    def send(chunk, targets):
-        for target in targets:
-            @pl.when(me != target)
-            def _():
-                out_copy(chunk, me, target).start()
+    def send(chunk, target):
+        out_copy(chunk, me, target).start()
 
     def keep(chunk):
         @pl.when(me != 0)
         def _():
-            out_ref[my_row, :, pl.ds(pl.multiple_of(my_off + chunk * CHUNK, CHUNK), CHUNK)] = x_out[chunk, me]
+            landed[my_row, :, pl.ds(pl.multiple_of(my_off + chunk * CHUNK, CHUNK), CHUNK)] = x_out[chunk, me]
 
     later = SWEEPS - 1
 
@@ -207,7 +206,8 @@
 
         @pl.when(jnp.logical_and(lax.rem(index, later) == later - 1, chunk < n_chunks - 1))
         def _():
-            send(chunk, range(1, n_time))
+            for target in range(1, n_time):
+                send(chunk, target)
             keep(chunk)
             integrate(chunk + 1)
         return carry
@@ -215,12 +215,11 @@
     integrate(0)
     lax.fori_loop(0, n_chunks * later - 1, sweep, 0)
     final = n_chunks - 1
-    state = initial(final)
-    begin = 1
-    for end in SEND_AFTER + (n_time,):
-        evaluate(sweep_items(final, range(begin, end), state))
-        send(final, range(begin, end))
-        begin = end
+    sends, begin = {}, 1
+    for end in SEND_AFTER + (n_time - 1,):
+        sends[end * n_blocks + LEAD + LAG] = [functools.partial(send, final, target) for target in range(begin, end + 1)]
+        begin = end + 1
+    evaluate(sweep_items(final, range(1, n_time), initial(final)), sends)
     keep(final)
 
     for slot in near_first:
@@ -229,19 +228,25 @@
 
     @pl.when(me == 0)
     def _():
-        pltpu.make_async_copy(x_ref, out_ref, whole_sem.at[0]).wait()
+        pltpu.make_async_copy(x_ref, landed.at[pl.ds(0, batch)], whole_sem.at[0]).wait()
 
     for chunk in range(n_chunks):
         for target in range(1, n_time):
-            @pl.when(me != target)
-            def _():
-                out_copy(chunk, me, target).wait_send()
+            out_copy(chunk, me, target).wait_send()
+
+    @pl.when(me != 1)
+    def _():
+        for chunk in range(n_chunks):
+            pair = me + 1 - 2 * lax.rem(me, 2)
+            out_copy(chunk, pair, pair).wait_recv()
 
     @pl.when(me != 0)
     def _():
         for chunk in range(n_chunks):
             for dist in range(1, n_time):
                 out_copy(chunk, lax.rem(me + dist, n_time), me).wait_recv()
+
+    out_ref[...] = landed[0:batch]
 
 
 def solution(mesh):
@@ -270,12 +275,13 @@
                 pltpu.VMEM((n_time, channels, CHUNK), jnp.bfloat16),
                 pltpu.VMEM((n_time, n_chunks, channels, CHUNK), jnp.float32),
                 pltpu.VMEM((n_chunks, n_time, channels, CHUNK), jnp.float32),
+                pltpu.VMEM((batch + 1, channels, tokens), jnp.float32),
                 pltpu.SemaphoreType.DMA((6,)),
                 pltpu.SemaphoreType.DMA((1,)),
                 pltpu.SemaphoreType.DMA((2, n_time)),
                 pltpu.SemaphoreType.DMA((2, n_time)),
                 pltpu.SemaphoreType.DMA((n_chunks, n_time)),
-                pltpu.SemaphoreType.DMA((n_chunks, n_time)),
+                pltpu.SemaphoreType.DMA((n_chunks, n_time + 1)),
             ],
             compiler_params=pltpu.CompilerParams(collective_id=0, has_side_effects=True, vmem_limit_bytes=48 * 2**20),
             name="picard",

time: 59.6 us -> 60.4 us (1.013)
  the two profiles are of different devices: /device:TPU:22 before, /device:TPU:21 now
where the time goes in v4:
time: 60.4 us; the launch traced here: 60.3 us
  Pallas kernels  58.8 us (97%)
  local copies, waits for them, and re-layouts  0.8 us (1%)
  between operations  0.66 us (1%)
    pallas_call x1, Pallas kernels, local(): pl.pallas_call(functools.partial(kernel_body, n_time), out_shape=jax.Shap...  58.8 us

profile of v4, /device:TPU:21, one launch (start us, length us, event | category | flops | bytes accessed | tf_op | source)
XLA Modules:
  0.0 60.3 jit_solution(10593026412713583084)
XLA Ops:
  0.7 58.8 %picard.1 = f32[8,16,1024]{2,1,0:T(8,128)S(1)} custom-call(f32[8,16,1024]{2,1,0:T(8,128)} %bitcast.6, bf16[16,1152]{1,0:T(8,128)(2,1)} %w_in_ref.1, bf16[16,1152]{1,0:T(8,128)(2,1)} %bitcast.7, bf16[1,1152]{1,0:T(2,128)(2,1)} %scale_ref.1, bf16[1,1152]{1,0:T(2,128)(2,1)} %shift_ref.1, f32[1]{0:T(128)S(6)} %copy.8.step_ref), custom_call_target="tpu_custom_call" | custom-call | tf_op jit(solution)/shard_map/picard/pallas_call | solution.py:260
  59.5 0.8 %copy.9 = f32[1,8,1024,16]{2,3,1,0:T(8,128)} copy(f32[1,8,1024,16]{2,3,1,0:T(8,128)S(1)} %bitcast.5) | data formatting | bytes 1048576

commit v5 on v3

--- a/solution.py
+++ b/solution.py
@@ -15,7 +15,9 @@
 LEAD = 1
 LAG = 1
 SEND_AFTER = (6, 11, 14)
-WAIT_AT = 1
+LENT = 9
+EARLY = 5
+AHEAD = 2
 
 
 def half_gelu_arg(half):
@@ -26,8 +28,8 @@
 
 
 def kernel_body(n_time, x_ref, w_in_ref, w_out_ref, scale_ref, shift_ref, step_ref, out_ref,
-                w_in, w_out, step_own, scale_own, shift_own, mods_all, step_all, weights, x_mine, x_half, drifts, x_out,
-                local_sem, whole_sem, mod_send, mod_recv, out_send, out_recv):
+                w_in, w_out, step_own, scale_own, shift_own, mods_all, step_all, weights, x_mine, x_whole, x_half, drifts, drift_out, x_out,
+                local_sem, whole_sem, mod_send, mod_recv, drift_send, drift_recv, out_send, out_recv):
     me = lax.axis_index("time")
     channels, hidden = w_in.shape
     batch, _, tokens = x_ref.shape
@@ -45,7 +47,7 @@
         pltpu.make_async_copy(src, dst, local_sem.at[slot])
         for slot, (src, dst) in enumerate((
             (scale_ref, scale_own), (shift_ref, shift_own), (step_ref, step_own), (w_in_ref, w_in), (w_out_ref, w_out),
-            (x_ref.at[my_row, :, pl.ds(pl.multiple_of(my_off, mine), mine)], x_mine)))
+            (x_ref.at[my_row, :, pl.ds(pl.multiple_of(my_off, mine), mine)], x_mine), (x_ref, x_whole)))
     ]
     for fetch in fetches:
         fetch.start()
@@ -137,28 +139,58 @@
             return slot, lambda: x_mine[:, columns(chunk)].astype(jnp.bfloat16), put
         return [item(slot, chunk) for slot in slots for chunk in range(n_chunks)]
 
-    prepare(0)
-    pl.semaphore_wait(barrier, n_time - 1)
-    for slot in near_first:
-        for copy in mod_copies(me, peer_of(slot), slot):
-            copy.start()
+    def lent_items(places):
+        def item(place, chunk):
+            row, off = spot(peer_of(near_first[place]))
+            def get():
+                return x_whole[row, :, pl.ds(pl.multiple_of(off + chunk * CHUNK, CHUNK), CHUNK)].astype(jnp.bfloat16)
+            def put(drift):
+                drift_out[place, chunk] = drift
+            return 0, get, put
+        return [item(place, chunk) for place in places for chunk in range(n_chunks)]
+
+    def drift_copy(place):
+        slot = near_first[place]
+        back = (n_chips - slot // 2) % n_chips * 2 + slot % 2
+        return pltpu.make_async_remote_copy(
+            src_ref=drift_out.at[place], dst_ref=drifts.at[back], send_sem=drift_send.at[place], recv_sem=drift_recv.at[back],
+            device_id={"time": peer_of(slot)}, device_id_type=pl.DeviceIdType.MESH)
+
+    def drift_arrival(slot):
+        return pltpu.make_async_remote_copy(
+            src_ref=drift_out.at[0], dst_ref=drifts.at[slot], send_sem=drift_send.at[0], recv_sem=drift_recv.at[slot],
+            device_id={"time": peer_of(slot)}, device_id_type=pl.DeviceIdType.MESH)
 
     def arrive(slots):
         for slot in slots:
             for copy in mod_copies(peer_of(slot), peer_of(slot), slot):
                 copy.wait_recv()
 
-    evaluate(first_items([0]))
-    near, middle = len(groups[0] + groups[1]), len(groups[2])
-    arrive(near_first[:near])
-    for slot in near_first[:near]:
+    prepare(0)
+    evaluate(first_items([0]) + lent_items(range(EARLY)))
+    pl.semaphore_wait(barrier, n_time - 1)
+    far, near = near_first[LENT:], near_first[:LENT]
+    for slot in far + near:
+        for copy in mod_copies(me, peer_of(slot), slot):
+            copy.start()
+    for place in range(EARLY):
+        drift_copy(place).start()
+    evaluate(lent_items(range(EARLY, LENT)))
+    for place in range(EARLY, LENT):
+        drift_copy(place).start()
+    per_slot = n_chunks * n_blocks
+    arrive(far[:AHEAD])
+    for slot in far[:AHEAD]:
         prepare(slot)
-    per_slot = n_chunks * n_blocks
-    extras = {WAIT_AT * per_slot: [functools.partial(arrive, near_first[near:near + middle])],
-              (WAIT_AT + middle) * per_slot: [functools.partial(arrive, near_first[near + middle:])]}
-    for place, slot in enumerate(near_first[near:]):
-        extras.setdefault((WAIT_AT + place) * per_slot + 1, []).append(functools.partial(prepare, slot))
-    evaluate(first_items(near_first), extras)
+    extras = {1: [functools.partial(arrive, far[AHEAD:])], (len(far) - AHEAD) * per_slot: [functools.partial(arrive, near)]}
+    for place, slot in enumerate(far[AHEAD:]):
+        extras.setdefault(place * per_slot + 2, []).append(functools.partial(prepare, slot))
+    rest = AHEAD * per_slot
+    for place, slot in enumerate(near):
+        extras.setdefault(min((len(far) - AHEAD) * per_slot + 1 + place * rest // len(near), len(far) * per_slot - 1), []).append(functools.partial(prepare, slot))
+    evaluate(first_items(far), extras)
+    for slot in near:
+        drift_arrival(slot).wait_recv()
 
     def integrate(chunk):
         last, x = drifts[slot_of(0), chunk], x_mine[:, columns(chunk)]
@@ -226,6 +258,8 @@
     for slot in near_first:
         for copy in mod_copies(me, peer_of(slot), slot):
             copy.wait_send()
+    for place in range(LENT):
+        drift_copy(place).wait_send()
 
     @pl.when(me == 0)
     def _():
@@ -267,13 +301,17 @@
                 pltpu.VMEM((n_time, 1, CHUNK), jnp.float32),
                 pltpu.VMEM((n_time, hidden, 4 * channels), jnp.bfloat16),
                 pltpu.VMEM((channels, mine), jnp.float32),
+                pltpu.VMEM((batch, channels, tokens), jnp.float32),
                 pltpu.VMEM((n_time, channels, CHUNK), jnp.bfloat16),
                 pltpu.VMEM((n_time, n_chunks, channels, CHUNK), jnp.float32),
+                pltpu.VMEM((LENT, n_chunks, channels, CHUNK), jnp.float32),
                 pltpu.VMEM((n_chunks, n_time, channels, CHUNK), jnp.float32),
-                pltpu.SemaphoreType.DMA((6,)),
+                pltpu.SemaphoreType.DMA((7,)),
                 pltpu.SemaphoreType.DMA((1,)),
                 pltpu.SemaphoreType.DMA((2, n_time)),
                 pltpu.SemaphoreType.DMA((2, n_time)),
+                pltpu.SemaphoreType.DMA((LENT,)),
+                pltpu.SemaphoreType.DMA((n_time,)),
                 pltpu.SemaphoreType.DMA((n_chunks, n_time)),
                 pltpu.SemaphoreType.DMA((n_chunks, n_time)),
             ],

time: 59.6 us -> 58.3 us (0.978)
  Pallas kernels: 58 us -> 56.7 us
    pallas_call x1, Pallas kernels: 58 us -> 56.7 us  [local(): pl.pallas_call(functools.partial(kernel_body, n_time), out_shape=jax.Shap...]
where the time goes in v5:
time: 58.3 us; the launch traced here: 58.2 us
  Pallas kernels  56.7 us (97%)
  local copies, waits for them, and re-layouts  0.8 us (1%)
  between operations  0.66 us (1%)
    pallas_call x1, Pallas kernels, local(): pl.pallas_call(functools.partial(kernel_body, n_time), out_shape=jax.Shap...  56.7 us

profile of v5, /device:TPU:22, one launch (start us, length us, event | category | flops | bytes accessed | tf_op | source)
XLA Modules:
  0.0 58.2 jit_solution(9261560282760618635)
XLA Ops:
  0.7 56.7 %picard.1 = f32[8,16,1024]{2,1,0:T(8,128)S(1)} custom-call(f32[8,16,1024]{2,1,0:T(8,128)} %bitcast.6, bf16[16,1152]{1,0:T(8,128)(2,1)} %w_in_ref.1, bf16[16,1152]{1,0:T(8,128)(2,1)} %bitcast.7, bf16[1,1152]{1,0:T(2,128)(2,1)} %scale_ref.1, bf16[1,1152]{1,0:T(2,128)(2,1)} %shift_ref.1, f32[1]{0:T(128)S(6)} %copy.8.step_ref), custom_call_target="tpu_custom_call" | custom-call | tf_op jit(solution)/shard_map/picard/pallas_call | solution.py:289
  57.4 0.8 %copy.9 = f32[1,8,1024,16]{2,3,1,0:T(8,128)} copy(f32[1,8,1024,16]{2,3,1,0:T(8,128)S(1)} %bitcast.5) | data formatting | bytes 1048576

commit v6 on v5

--- a/solution.py
+++ b/solution.py
@@ -16,7 +16,7 @@
 LAG = 1
 SEND_AFTER = (6, 11, 14)
 LENT = 9
-EARLY = 5
+EARLY = 2
 AHEAD = 2
 
 
@@ -175,10 +175,15 @@
             copy.start()
     for place in range(EARLY):
         drift_copy(place).start()
-    evaluate(lent_items(range(EARLY, LENT)))
-    for place in range(EARLY, LENT):
-        drift_copy(place).start()
     per_slot = n_chunks * n_blocks
+
+    def lend(places):
+        for place in places:
+            drift_copy(place).start()
+
+    half = (LENT - EARLY) // 2
+    evaluate(lent_items(range(EARLY, LENT)), {half * per_slot + LEAD + LAG: [functools.partial(lend, range(EARLY, EARLY + half))]})
+    lend(range(EARLY + half, LENT))
     arrive(far[:AHEAD])
     for slot in far[:AHEAD]:
         prepare(slot)

time: 58.3 us -> 56.9 us (0.976)
  the two profiles are of different devices: /device:TPU:22 before, /device:TPU:21 now
where the time goes in v6:
time: 56.9 us; the launch traced here: 56.5 us
  Pallas kernels  55 us (97%)
  local copies, waits for them, and re-layouts  0.8 us (1%)
  between operations  0.66 us (1%)
    pallas_call x1, Pallas kernels, local(): pl.pallas_call(functools.partial(kernel_body, n_time), out_shape=jax.Shap...  55 us

profile of v6, /device:TPU:21, one launch (start us, length us, event | category | flops | bytes accessed | tf_op | source)
XLA Modules:
  0.0 56.5 jit_solution(1194106946581513248)
XLA Ops:
  0.7 55.0 %picard.1 = f32[8,16,1024]{2,1,0:T(8,128)S(1)} custom-call(f32[8,16,1024]{2,1,0:T(8,128)} %bitcast.6, bf16[16,1152]{1,0:T(8,128)(2,1)} %w_in_ref.1, bf16[16,1152]{1,0:T(8,128)(2,1)} %bitcast.7, bf16[1,1152]{1,0:T(2,128)(2,1)} %scale_ref.1, bf16[1,1152]{1,0:T(2,128)(2,1)} %shift_ref.1, f32[1]{0:T(128)S(6)} %copy.8.step_ref), custom_call_target="tpu_custom_call" | custom-call | tf_op jit(solution)/shard_map/picard/pallas_call | solution.py:294
  55.7 0.8 %copy.9 = f32[1,8,1024,16]{2,3,1,0:T(8,128)} copy(f32[1,8,1024,16]{2,3,1,0:T(8,128)S(1)} %bitcast.5) | data formatting | bytes 1048576

commit v7 on v6

--- a/solution.py
+++ b/solution.py
@@ -14,7 +14,7 @@
 BLOCK = 384
 LEAD = 1
 LAG = 1
-SEND_AFTER = (6, 11, 14)
+SEND_AFTER = (4, 8, 11, 13, 14)
 LENT = 9
 EARLY = 2
 AHEAD = 2
@@ -28,7 +28,7 @@
 
 
 def kernel_body(n_time, x_ref, w_in_ref, w_out_ref, scale_ref, shift_ref, step_ref, out_ref,
-                w_in, w_out, step_own, scale_own, shift_own, mods_all, step_all, weights, x_mine, x_whole, x_half, drifts, drift_out, x_out,
+                w_in, w_out, step_own, scale_own, shift_own, mods_all, step_all, weights, x_mine, x_whole, x_half, drifts, drift_out, x_out, landed,
                 local_sem, whole_sem, mod_send, mod_recv, drift_send, drift_recv, out_send, out_recv):
     me = lax.axis_index("time")
     channels, hidden = w_in.shape
@@ -76,7 +76,7 @@
 
     @pl.when(me == 0)
     def _():
-        pltpu.make_async_copy(x_ref, out_ref, whole_sem.at[0]).start()
+        pltpu.make_async_copy(x_ref, landed.at[pl.ds(0, batch)], whole_sem.at[0]).start()
 
     def mod_copies(source, target, slot):
         return [
@@ -119,14 +119,14 @@
             if block == n_blocks - 1:
                 items[item][2](drift.pop(item))
 
-        for index in range(len(blocks) + LEAD + LAG):
+        for index in range(len(blocks) + LEAD + LAG + 1):
+            for extra in extras.get(index, ()):
+                extra()
             if index < len(blocks):
-                for extra in extras.get(index, ()):
-                    extra()
                 project(index)
             if LEAD <= index < len(blocks) + LEAD:
                 act[index - LEAD] = half_gelu_arg(pre.pop(index - LEAD))
-            if index >= LEAD + LAG:
+            if LEAD + LAG <= index < len(blocks) + LEAD + LAG:
                 contract(index - LEAD - LAG)
 
     def columns(chunk):
@@ -208,9 +208,11 @@
     def out_copy(chunk, source, target):
         row, off = spot(source)
         cols = pl.ds(pl.multiple_of(off + chunk * CHUNK, CHUNK), CHUNK)
+        own = source == target
         return pltpu.make_async_remote_copy(
-            src_ref=x_out.at[chunk, target], dst_ref=out_ref.at[row, :, cols], send_sem=out_send.at[chunk, target],
-            recv_sem=out_recv.at[chunk, source], device_id={"time": target}, device_id_type=pl.DeviceIdType.MESH)
+            src_ref=x_out.at[chunk, target], dst_ref=landed.at[jnp.where(own, batch, row), :, cols], send_sem=out_send.at[chunk, target],
+            recv_sem=out_recv.at[chunk, jnp.where(own, n_time, source)], device_id={"time": jnp.where(own, target + 1 - 2 * lax.rem(target, 2), target)},
+            device_id_type=pl.DeviceIdType.MESH)
 
     def sweep_items(chunk, steps, state):
         def item(step):
@@ -225,16 +227,13 @@
     def initial(chunk):
         return {"last": drifts[slot_of(0), chunk], "x": x_mine[:, columns(chunk)]}
 
-    def send(chunk, targets):
-        for target in targets:
-            @pl.when(me != target)
-            def _():
-                out_copy(chunk, me, target).start()
+    def send(chunk, target):
+        out_copy(chunk, me, target).start()
 
     def keep(chunk):
         @pl.when(me != 0)
         def _():
-            out_ref[my_row, :, pl.ds(pl.multiple_of(my_off + chunk * CHUNK, CHUNK), CHUNK)] = x_out[chunk, me]
+            landed[my_row, :, pl.ds(pl.multiple_of(my_off + chunk * CHUNK, CHUNK), CHUNK)] = x_out[chunk, me]
 
     later = SWEEPS - 1
 
@@ -244,7 +243,8 @@
 
         @pl.when(jnp.logical_and(lax.rem(index, later) == later - 1, chunk < n_chunks - 1))
         def _():
-            send(chunk, range(1, n_time))
+            for target in range(1, n_time):
+                send(chunk, target)
             keep(chunk)
             integrate(chunk + 1)
         return carry
@@ -252,12 +252,11 @@
     integrate(0)
     lax.fori_loop(0, n_chunks * later - 1, sweep, 0)
     final = n_chunks - 1
-    state = initial(final)
-    begin = 1
-    for end in SEND_AFTER + (n_time,):
-        evaluate(sweep_items(final, range(begin, end), state))
-        send(final, range(begin, end))
-        begin = end
+    sends, begin = {}, 1
+    for end in SEND_AFTER + (n_time - 1,):
+        sends[end * n_blocks + LEAD + LAG] = [functools.partial(send, final, target) for target in range(begin, end + 1)]
+        begin = end + 1
+    evaluate(sweep_items(final, range(1, n_time), initial(final)), sends)
     keep(final)
 
     for slot in near_first:
@@ -268,19 +267,25 @@
 
     @pl.when(me == 0)
     def _():
-        pltpu.make_async_copy(x_ref, out_ref, whole_sem.at[0]).wait()
+        pltpu.make_async_copy(x_ref, landed.at[pl.ds(0, batch)], whole_sem.at[0]).wait()
 
     for chunk in range(n_chunks):
         for target in range(1, n_time):
-            @pl.when(me != target)
-            def _():
-                out_copy(chunk, me, target).wait_send()
+            out_copy(chunk, me, target).wait_send()
+
+    @pl.when(me != 1)
+    def _():
+        for chunk in range(n_chunks):
+            pair = me + 1 - 2 * lax.rem(me, 2)
+            out_copy(chunk, pair, pair).wait_recv()
 
     @pl.when(me != 0)
     def _():
         for chunk in range(n_chunks):
             for dist in range(1, n_time):
                 out_copy(chunk, lax.rem(me + dist, n_time), me).wait_recv()
+
+    out_ref[...] = landed[0:batch]
 
 
 def solution(mesh):
@@ -311,6 +316,7 @@
                 pltpu.VMEM((n_time, n_chunks, channels, CHUNK), jnp.float32),
                 pltpu.VMEM((LENT, n_chunks, channels, CHUNK), jnp.float32),
                 pltpu.VMEM((n_chunks, n_time, channels, CHUNK), jnp.float32),
+                pltpu.VMEM((batch + 1, channels, tokens), jnp.float32),
                 pltpu.SemaphoreType.DMA((7,)),
                 pltpu.SemaphoreType.DMA((1,)),
                 pltpu.SemaphoreType.DMA((2, n_time)),
@@ -318,7 +324,7 @@
                 pltpu.SemaphoreType.DMA((LENT,)),
                 pltpu.SemaphoreType.DMA((n_time,)),
                 pltpu.SemaphoreType.DMA((n_chunks, n_time)),
-                pltpu.SemaphoreType.DMA((n_chunks, n_time)),
+                pltpu.SemaphoreType.DMA((n_chunks, n_time + 1)),
             ],
             compiler_params=pltpu.CompilerParams(collective_id=0, has_side_effects=True, vmem_limit_bytes=48 * 2**20),
             name="picard",

time: 56.9 us -> 55.6 us (0.977)
  Pallas kernels: 55 us -> 54.1 us
    pallas_call x1, Pallas kernels: 55 us -> 54.1 us  [local(): pl.pallas_call(functools.partial(kernel_body, n_time), out_shape=jax.Shap...]
where the time goes in v7:
time: 55.6 us; the launch traced here: 55.5 us
  Pallas kernels  54.1 us (97%)
  local copies, waits for them, and re-layouts  0.8 us (1%)
  between operations  0.66 us (1%)
    pallas_call x1, Pallas kernels, local(): pl.pallas_call(functools.partial(kernel_body, n_time), out_shape=jax.Shap...  54.1 us

profile of v7, /device:TPU:21, one launch (start us, length us, event | category | flops | bytes accessed | tf_op | source)
XLA Modules:
  0.0 55.5 jit_solution(1643357718184879764)
XLA Ops:
  0.7 54.1 %picard.1 = f32[8,16,1024]{2,1,0:T(8,128)S(1)} custom-call(f32[8,16,1024]{2,1,0:T(8,128)} %bitcast.6, bf16[16,1152]{1,0:T(8,128)(2,1)} %w_in_ref.1, bf16[16,1152]{1,0:T(8,128)(2,1)} %bitcast.7, bf16[1,1152]{1,0:T(2,128)(2,1)} %scale_ref.1, bf16[1,1152]{1,0:T(2,128)(2,1)} %shift_ref.1, f32[1]{0:T(128)S(6)} %copy.8.step_ref), custom_call_target="tpu_custom_call" | custom-call | tf_op jit(solution)/shard_map/picard/pallas_call | solution.py:299
  54.7 0.8 %copy.9 = f32[1,8,1024,16]{2,3,1,0:T(8,128)} copy(f32[1,8,1024,16]{2,3,1,0:T(8,128)S(1)} %bitcast.5) | data formatting | bytes 1048576
